TPU v7x, 128 devices: a whole 4x4x4 slice. The times are simulated.
128 devices in a mesh: ens: 1, col: 16 (over z, y), row: 8 (over x, core).
Axes of the slice: x: 4, y: 4, z: 4, core: 2. Of those that a mesh axis runs over, the one named last changes fastest.
Arguments:
- images: bfloat16 [32, 64, 512, 256], P('ens', 'row', 'col')
- w_conv: bfloat16 [4, 3, 3, 256, 256], replicated
- b_conv: float32 [4, 256], replicated
Outputs:
- output: bfloat16 [32, 64, 512, 256], P('ens', 'row', 'col')
All inputs are finite; a program needn't handle non-finite values.
Results may differ from a plain program's by a relative error of at most 0.00389.
Values are sent between devices in bfloat16 or wider.
A program may use at most 1 GiB of HBM per device.

v0:
```python
import jax
import jax.numpy as jnp
from jax import lax
from jax.sharding import PartitionSpec as P

CONV_DIMS = ("NHWC", "HWIO", "NHWC")


def edge_exchange(x_tile, axis_name, to_next, to_prev, axis_dim):
    edge_len = x_tile.shape[axis_dim]
    head_edge = lax.slice_in_dim(x_tile, 0, 1, axis=axis_dim)
    tail_edge = lax.slice_in_dim(x_tile, edge_len - 1, edge_len, axis=axis_dim)
    from_prev = lax.ppermute(tail_edge, axis_name, perm=to_next)
    from_next = lax.ppermute(head_edge, axis_name, perm=to_prev)
    return jnp.concatenate([from_prev, x_tile, from_next], axis=axis_dim)


def solution(mesh):
    row_devs = mesh.shape["row"]
    col_devs = mesh.shape["col"]
    row_next = [(index, index + 1) for index in range(row_devs - 1)]
    row_prev = [(index + 1, index) for index in range(row_devs - 1)]
    col_next = [(index, index + 1) for index in range(col_devs - 1)]
    col_prev = [(index + 1, index) for index in range(col_devs - 1)]
    act_spec = P("ens", "row", "col", None)

    def local_stack(x_tile, weights, biases):
        hidden = x_tile
        for layer_idx in range(weights.shape[0]):
            padded = edge_exchange(hidden, "row", row_next, row_prev, 1)
            padded = edge_exchange(padded, "col", col_next, col_prev, 2)
            summed = lax.conv_general_dilated(padded, weights[layer_idx], (1, 1), "VALID", dimension_numbers=CONV_DIMS, preferred_element_type=jnp.float32)
            hidden = jnp.maximum(summed + biases[layer_idx], 0.0).astype(jnp.bfloat16)
        return hidden

    return jax.shard_map(local_stack, mesh=mesh, in_specs=(act_spec, P(), P()), out_specs=act_spec, check_vma=False)
```

profile of v0, /device:TPU:26, one launch (start us, length us, event | category | flops | bytes accessed | tf_op | source)
XLA Modules:
  0.0 150.0 jit_solution(5628728924235309088)
XLA Ops:
  0.0 1.4 fusion.60
  1.4 0.3 copy.9
  1.7 1.9 %collective-permute-start = (bf16[32,1,32,256]{3,0,2,1:T(8,128)(2,1)S(1)}, bf16[32,1,32,256]{3,0,2,1:T(8,128)(2,1)S(1)}, u32[]{:S(2)}, u32[]{:S(2)}) collective-permute-start(bf16[32,1,32,256]{3,0,2,1:T(8,128)(2,1)S(1)} %copy.9), channel_id=1, source_target_pairs={{0,1},{1,2},{2,3},{3,4},{4,5},{5,6},{6,7},{8,9},{9,10},{10,11},{11... | collective-permute-start | bytes 1572872 | tf_op jit(solution)/shard_map/ppermute | solution.py:13
  3.7 0.3 copy.10
  4.0 3.6 %collective-permute-start.1 = (bf16[32,1,32,256]{3,0,2,1:T(8,128)(2,1)S(1)}, bf16[32,1,32,256]{3,0,2,1:T(8,128)(2,1)S(1)}, u32[]{:S(2)}, u32[]{:S(2)}) collective-permute-start(bf16[32,1,32,256]{3,0,2,1:T(8,128)(2,1)S(1)} %copy.10), channel_id=1, source_target_pairs={{1,0},{2,1},{3,2},{4,3},{5,4},{6,5},{7,6},{9,8},{10,9},{11,10},{12... | collective-permute-start | bytes 1572872 | tf_op jit(solution)/shard_map/ppermute | solution.py:14
  7.6 4.6 %collective-permute-done = bf16[32,1,32,256]{3,0,2,1:T(8,128)(2,1)S(1)} collective-permute-done((bf16[32,1,32,256]{3,0,2,1:T(8,128)(2,1)S(1)}, bf16[32,1,32,256]{3,0,2,1:T(8,128)(2,1)S(1)}, u32[]{:S(2)}, u32[]{:S(2)}) %collective-permute-start) | collective-permute-done | bytes 524320 | tf_op jit(solution)/shard_map/ppermute | solution.py:13
  12.3 0.0 copy-done
  12.3 0.0 copy-start.1
  12.3 0.0 slice-start.1
  12.3 2.6 %constant_dynamic-update-slice_fusion.1 = bf16[32,10,32,256]{3,0,2,1:T(8,128)(2,1)S(1)} fusion(bf16[32,10,32,256]{3,0,2,1:T(8,128)(2,1)S(1)} %constant_dynamic-update-slice_fusion.2, bf16[32,8,32,256]{3,2,1,0:T(8,128)(2,1)S(1)} %copy-done), kind=kLoop, calls=%fused_computation.58 | loop fusion | bytes 8388608
  14.9 0.0 collective-permute-done.1
  15.0 3.5 %collective-permute-start.2 = (bf16[32,10,1,256]{3,0,2,1:T(8,128)(2,1)S(1)}, bf16[32,10,1,256]{3,0,2,1:T(8,128)(2,1)S(1)}, u32[]{:S(2)}, u32[]{:S(2)}) collective-permute-start(bf16[32,10,1,256]{3,0,2,1:T(8,128)(2,1)S(1)} %get-tuple-element.11), channel_id=1, source_target_pairs={{0,8},{8,16},{16,24},{24,32},{32,40},{40,48},{48,56},{56,64},{64,7... | collective-permute-start | bytes 491528 | tf_op jit(solution)/shard_map/ppermute | solution.py:13
  18.5 2.4 %collective-permute-start.3 = (bf16[32,10,1,256]{3,0,2,1:T(8,128)(2,1)S(1)}, bf16[32,10,1,256]{3,0,2,1:T(8,128)(2,1)S(1)}, u32[]{:S(2)}, u32[]{:S(2)}) collective-permute-start(bf16[32,10,1,256]{3,0,2,1:T(8,128)(2,1)S(1)} %get-tuple-element.12), channel_id=1, source_target_pairs={{8,0},{16,8},{24,16},{32,24},{40,32},{48,40},{56,48},{64,56},{72,6... | collective-permute-start | bytes 491528 | tf_op jit(solution)/shard_map/ppermute | solution.py:14
  20.9 0.0 copy-done.1
  20.9 2.9 %collective-permute-done.2 = bf16[32,10,1,256]{3,0,2,1:T(8,128)(2,1)S(1)} collective-permute-done((bf16[32,10,1,256]{3,0,2,1:T(8,128)(2,1)S(1)}, bf16[32,10,1,256]{3,0,2,1:T(8,128)(2,1)S(1)}, u32[]{:S(2)}, u32[]{:S(2)}) %collective-permute-start.2) | collective-permute-done | bytes 163872 | tf_op jit(solution)/shard_map/ppermute | solution.py:13
  23.8 5.8 %collective-permute-done.3 = bf16[32,10,1,256]{3,0,2,1:T(8,128)(2,1)S(1)} collective-permute-done((bf16[32,10,1,256]{3,0,2,1:T(8,128)(2,1)S(1)}, bf16[32,10,1,256]{3,0,2,1:T(8,128)(2,1)S(1)}, u32[]{:S(2)}, u32[]{:S(2)}) %collective-permute-start.3) | collective-permute-done | bytes 163872 | tf_op jit(solution)/shard_map/ppermute | solution.py:14
  29.6 10.2 %maximum_convert_fusion.3 = bf16[32,8,32,256]{3,0,2,1:T(8,128)(2,1)S(1)} fusion(f32[256]{0:T(256)S(1)} %bitcast.19, bf16[32,10,1,256]{3,0,2,1:T(8,128)(2,1)S(1)} %collective-permute-done.3, bf16[32,10,32,256]{3,0,2,1:T(8,128)(2,1)S(1)} %constant_dynamic-update-slice_fusion, bf16[32,10,1,256]{3,0,2,1:T(8,128)(2,1)S(1)} %collective-permute-done.2, ...), kind=kOutput, calls=%fused_computation.3 | convolution fusion | flops 9675538432 | bytes 10945536 | tf_op jit(solution)/shard_map/conv_general_dilated | solution.py:32
  39.8 0.1 fusion.59
  39.9 1.9 %collective-permute-start.4 = (bf16[32,1,32,256]{3,0,2,1:T(8,128)(2,1)S(1)}, bf16[32,1,32,256]{3,0,2,1:T(8,128)(2,1)S(1)}, u32[]{:S(2)}, u32[]{:S(2)}) collective-permute-start(bf16[32,1,32,256]{3,0,2,1:T(8,128)(2,1)S(1)} %get-tuple-element.17), channel_id=1, source_target_pairs={{0,1},{1,2},{2,3},{3,4},{4,5},{5,6},{6,7},{8,9},{9,10},{10,11},{11... | collective-permute-start | bytes 1572872 | tf_op jit(solution)/shard_map/ppermute | solution.py:13
  41.8 3.6 %collective-permute-start.5 = (bf16[32,1,32,256]{3,0,2,1:T(8,128)(2,1)S(1)}, bf16[32,1,32,256]{3,0,2,1:T(8,128)(2,1)S(1)}, u32[]{:S(2)}, u32[]{:S(2)}) collective-permute-start(bf16[32,1,32,256]{3,0,2,1:T(8,128)(2,1)S(1)} %get-tuple-element.18), channel_id=1, source_target_pairs={{1,0},{2,1},{3,2},{4,3},{5,4},{6,5},{7,6},{9,8},{10,9},{11,10},{12... | collective-permute-start | bytes 1572872 | tf_op jit(solution)/shard_map/ppermute | solution.py:14
  45.5 4.9 %collective-permute-done.4 = bf16[32,1,32,256]{3,0,2,1:T(8,128)(2,1)S(1)} collective-permute-done((bf16[32,1,32,256]{3,0,2,1:T(8,128)(2,1)S(1)}, bf16[32,1,32,256]{3,0,2,1:T(8,128)(2,1)S(1)}, u32[]{:S(2)}, u32[]{:S(2)}) %collective-permute-start.4) | collective-permute-done | bytes 524320 | tf_op jit(solution)/shard_map/ppermute | solution.py:13
  50.4 1.7 %collective-permute-done.5 = bf16[32,1,32,256]{3,0,2,1:T(8,128)(2,1)S(1)} collective-permute-done((bf16[32,1,32,256]{3,0,2,1:T(8,128)(2,1)S(1)}, bf16[32,1,32,256]{3,0,2,1:T(8,128)(2,1)S(1)}, u32[]{:S(2)}, u32[]{:S(2)}) %collective-permute-start.5) | collective-permute-done | bytes 524320 | tf_op jit(solution)/shard_map/ppermute | solution.py:14
  52.2 1.9 %collective-permute-start.6 = (bf16[32,10,1,256]{3,0,2,1:T(8,128)(2,1)S(1)}, bf16[32,10,1,256]{3,0,2,1:T(8,128)(2,1)S(1)}, u32[]{:S(2)}, u32[]{:S(2)}) collective-permute-start(bf16[32,10,1,256]{3,0,2,1:T(8,128)(2,1)S(1)} %get-tuple-element.9), channel_id=1, source_target_pairs={{0,8},{8,16},{16,24},{24,32},{32,40},{40,48},{48,56},{56,64},{64,7... | collective-permute-start | bytes 491528 | tf_op jit(solution)/shard_map/ppermute | solution.py:13
  54.1 4.1 %collective-permute-start.7 = (bf16[32,10,1,256]{3,0,2,1:T(8,128)(2,1)S(1)}, bf16[32,10,1,256]{3,0,2,1:T(8,128)(2,1)S(1)}, u32[]{:S(2)}, u32[]{:S(2)}) collective-permute-start(bf16[32,10,1,256]{3,0,2,1:T(8,128)(2,1)S(1)} %get-tuple-element.10), channel_id=1, source_target_pairs={{8,0},{16,8},{24,16},{32,24},{40,32},{48,40},{56,48},{64,56},{72,6... | collective-permute-start | bytes 491528 | tf_op jit(solution)/shard_map/ppermute | solution.py:14
  58.2 2.3 %collective-permute-done.6 = bf16[32,10,1,256]{3,0,2,1:T(8,128)(2,1)S(1)} collective-permute-done((bf16[32,10,1,256]{3,0,2,1:T(8,128)(2,1)S(1)}, bf16[32,10,1,256]{3,0,2,1:T(8,128)(2,1)S(1)}, u32[]{:S(2)}, u32[]{:S(2)}) %collective-permute-start.6) | collective-permute-done | bytes 163872 | tf_op jit(solution)/shard_map/ppermute | solution.py:13
  60.5 4.0 %collective-permute-done.7 = bf16[32,10,1,256]{3,0,2,1:T(8,128)(2,1)S(1)} collective-permute-done((bf16[32,10,1,256]{3,0,2,1:T(8,128)(2,1)S(1)}, bf16[32,10,1,256]{3,0,2,1:T(8,128)(2,1)S(1)}, u32[]{:S(2)}, u32[]{:S(2)}) %collective-permute-start.7) | collective-permute-done | bytes 163872 | tf_op jit(solution)/shard_map/ppermute | solution.py:14
  64.5 10.2 %maximum_convert_fusion.2 = bf16[32,8,32,256]{3,0,2,1:T(8,128)(2,1)S(1)} fusion(bf16[32,10,1,256]{3,0,2,1:T(8,128)(2,1)S(1)} %collective-permute-done.7, bf16[32,1,32,256]{3,0,2,1:T(8,128)(2,1)S(1)} %collective-permute-done.5, bf16[32,8,32,256]{3,0,2,1:T(8,128)(2,1)S(1)} %maximum_convert_fusion.3, bf16[32,1,32,256]{3,0,2,1:T(8,128)(2,1)S(1)} %collective-permute-done.4, ...), kind=kOutput, calls=%fused_computation.2 | convolution fusion | flops 9681108992 | bytes 10945536 | tf_op jit(solution)/shard_map/conv_general_dilated | solution.py:32
  74.8 0.1 fusion.58
  74.9 2.6 %collective-permute-start.8 = (bf16[32,1,32,256]{3,0,2,1:T(8,128)(2,1)S(1)}, bf16[32,1,32,256]{3,0,2,1:T(8,128)(2,1)S(1)}, u32[]{:S(2)}, u32[]{:S(2)}) collective-permute-start(bf16[32,1,32,256]{3,0,2,1:T(8,128)(2,1)S(1)} %get-tuple-element.15), channel_id=1, source_target_pairs={{0,1},{1,2},{2,3},{3,4},{4,5},{5,6},{6,7},{8,9},{9,10},{10,11},{11... | collective-permute-start | bytes 1572872 | tf_op jit(solution)/shard_map/ppermute | solution.py:13
  77.5 2.9 %collective-permute-start.9 = (bf16[32,1,32,256]{3,0,2,1:T(8,128)(2,1)S(1)}, bf16[32,1,32,256]{3,0,2,1:T(8,128)(2,1)S(1)}, u32[]{:S(2)}, u32[]{:S(2)}) collective-permute-start(bf16[32,1,32,256]{3,0,2,1:T(8,128)(2,1)S(1)} %get-tuple-element.16), channel_id=1, source_target_pairs={{1,0},{2,1},{3,2},{4,3},{5,4},{6,5},{7,6},{9,8},{10,9},{11,10},{12... | collective-permute-start | bytes 1572872 | tf_op jit(solution)/shard_map/ppermute | solution.py:14
  80.4 4.9 %collective-permute-done.8 = bf16[32,1,32,256]{3,0,2,1:T(8,128)(2,1)S(1)} collective-permute-done((bf16[32,1,32,256]{3,0,2,1:T(8,128)(2,1)S(1)}, bf16[32,1,32,256]{3,0,2,1:T(8,128)(2,1)S(1)}, u32[]{:S(2)}, u32[]{:S(2)}) %collective-permute-start.8) | collective-permute-done | bytes 524320 | tf_op jit(solution)/shard_map/ppermute | solution.py:13
  85.4 1.7 %collective-permute-done.9 = bf16[32,1,32,256]{3,0,2,1:T(8,128)(2,1)S(1)} collective-permute-done((bf16[32,1,32,256]{3,0,2,1:T(8,128)(2,1)S(1)}, bf16[32,1,32,256]{3,0,2,1:T(8,128)(2,1)S(1)}, u32[]{:S(2)}, u32[]{:S(2)}) %collective-permute-start.9) | collective-permute-done | bytes 524320 | tf_op jit(solution)/shard_map/ppermute | solution.py:14
  87.2 1.9 %collective-permute-start.10 = (bf16[32,10,1,256]{3,0,2,1:T(8,128)(2,1)S(1)}, bf16[32,10,1,256]{3,0,2,1:T(8,128)(2,1)S(1)}, u32[]{:S(2)}, u32[]{:S(2)}) collective-permute-start(bf16[32,10,1,256]{3,0,2,1:T(8,128)(2,1)S(1)} %get-tuple-element.7), channel_id=1, source_target_pairs={{0,8},{8,16},{16,24},{24,32},{32,40},{40,48},{48,56},{56,64},{64,7... | collective-permute-start | bytes 491528 | tf_op jit(solution)/shard_map/ppermute | solution.py:13
  89.1 3.9 %collective-permute-start.11 = (bf16[32,10,1,256]{3,0,2,1:T(8,128)(2,1)S(1)}, bf16[32,10,1,256]{3,0,2,1:T(8,128)(2,1)S(1)}, u32[]{:S(2)}, u32[]{:S(2)}) collective-permute-start(bf16[32,10,1,256]{3,0,2,1:T(8,128)(2,1)S(1)} %get-tuple-element.8), channel_id=1, source_target_pairs={{8,0},{16,8},{24,16},{32,24},{40,32},{48,40},{56,48},{64,56},{72,6... | collective-permute-start | bytes 491528 | tf_op jit(solution)/shard_map/ppermute | solution.py:14
  93.0 2.6 %collective-permute-done.10 = bf16[32,10,1,256]{3,0,2,1:T(8,128)(2,1)S(1)} collective-permute-done((bf16[32,10,1,256]{3,0,2,1:T(8,128)(2,1)S(1)}, bf16[32,10,1,256]{3,0,2,1:T(8,128)(2,1)S(1)}, u32[]{:S(2)}, u32[]{:S(2)}) %collective-permute-start.10) | collective-permute-done | bytes 163872 | tf_op jit(solution)/shard_map/ppermute | solution.py:13
  95.6 4.0 %collective-permute-done.11 = bf16[32,10,1,256]{3,0,2,1:T(8,128)(2,1)S(1)} collective-permute-done((bf16[32,10,1,256]{3,0,2,1:T(8,128)(2,1)S(1)}, bf16[32,10,1,256]{3,0,2,1:T(8,128)(2,1)S(1)}, u32[]{:S(2)}, u32[]{:S(2)}) %collective-permute-start.11) | collective-permute-done | bytes 163872 | tf_op jit(solution)/shard_map/ppermute | solution.py:14
  99.6 10.3 %maximum_convert_fusion.1 = bf16[32,8,32,256]{3,0,2,1:T(8,128)(2,1)S(1)} fusion(bf16[32,10,1,256]{3,0,2,1:T(8,128)(2,1)S(1)} %collective-permute-done.11, bf16[32,1,32,256]{3,0,2,1:T(8,128)(2,1)S(1)} %collective-permute-done.9, bf16[32,8,32,256]{3,0,2,1:T(8,128)(2,1)S(1)} %maximum_convert_fusion.2, bf16[32,1,32,256]{3,0,2,1:T(8,128)(2,1)S(1)} %collective-permute-done.8, ...), kind=kOutput, calls=%fused_computation.1 | convolution fusion | flops 9681108992 | bytes 10945536 | tf_op jit(solution)/shard_map/conv_general_dilated | solution.py:32
  109.9 0.1 fusion.57
  110.0 2.5 %collective-permute-start.12 = (bf16[32,1,32,256]{3,0,2,1:T(8,128)(2,1)S(1)}, bf16[32,1,32,256]{3,0,2,1:T(8,128)(2,1)S(1)}, u32[]{:S(2)}, u32[]{:S(2)}) collective-permute-start(bf16[32,1,32,256]{3,0,2,1:T(8,128)(2,1)S(1)} %get-tuple-element.13), channel_id=1, source_target_pairs={{0,1},{1,2},{2,3},{3,4},{4,5},{5,6},{6,7},{8,9},{9,10},{10,11},{11... | collective-permute-start | bytes 1572872 | tf_op jit(solution)/shard_map/ppermute | solution.py:13
  112.5 3.0 %collective-permute-start.13 = (bf16[32,1,32,256]{3,0,2,1:T(8,128)(2,1)S(1)}, bf16[32,1,32,256]{3,0,2,1:T(8,128)(2,1)S(1)}, u32[]{:S(2)}, u32[]{:S(2)}) collective-permute-start(bf16[32,1,32,256]{3,0,2,1:T(8,128)(2,1)S(1)} %get-tuple-element.14), channel_id=1, source_target_pairs={{1,0},{2,1},{3,2},{4,3},{5,4},{6,5},{7,6},{9,8},{10,9},{11,10},{12... | collective-permute-start | bytes 1572872 | tf_op jit(solution)/shard_map/ppermute | solution.py:14
  115.5 4.9 %collective-permute-done.12 = bf16[32,1,32,256]{3,0,2,1:T(8,128)(2,1)S(1)} collective-permute-done((bf16[32,1,32,256]{3,0,2,1:T(8,128)(2,1)S(1)}, bf16[32,1,32,256]{3,0,2,1:T(8,128)(2,1)S(1)}, u32[]{:S(2)}, u32[]{:S(2)}) %collective-permute-start.12) | collective-permute-done | bytes 524320 | tf_op jit(solution)/shard_map/ppermute | solution.py:13
  120.5 1.7 %collective-permute-done.13 = bf16[32,1,32,256]{3,0,2,1:T(8,128)(2,1)S(1)} collective-permute-done((bf16[32,1,32,256]{3,0,2,1:T(8,128)(2,1)S(1)}, bf16[32,1,32,256]{3,0,2,1:T(8,128)(2,1)S(1)}, u32[]{:S(2)}, u32[]{:S(2)}) %collective-permute-start.13) | collective-permute-done | bytes 524320 | tf_op jit(solution)/shard_map/ppermute | solution.py:14
  122.2 2.1 %collective-permute-start.14 = (bf16[32,10,1,256]{3,0,2,1:T(8,128)(2,1)S(1)}, bf16[32,10,1,256]{3,0,2,1:T(8,128)(2,1)S(1)}, u32[]{:S(2)}, u32[]{:S(2)}) collective-permute-start(bf16[32,10,1,256]{3,0,2,1:T(8,128)(2,1)S(1)} %get-tuple-element.5), channel_id=1, source_target_pairs={{0,8},{8,16},{16,24},{24,32},{32,40},{40,48},{48,56},{56,64},{64,7... | collective-permute-start | bytes 491528 | tf_op jit(solution)/shard_map/ppermute | solution.py:13
  124.4 3.9 %collective-permute-start.15 = (bf16[32,10,1,256]{3,0,2,1:T(8,128)(2,1)S(1)}, bf16[32,10,1,256]{3,0,2,1:T(8,128)(2,1)S(1)}, u32[]{:S(2)}, u32[]{:S(2)}) collective-permute-start(bf16[32,10,1,256]{3,0,2,1:T(8,128)(2,1)S(1)} %get-tuple-element.6), channel_id=1, source_target_pairs={{8,0},{16,8},{24,16},{32,24},{40,32},{48,40},{56,48},{64,56},{72,6... | collective-permute-start | bytes 491528 | tf_op jit(solution)/shard_map/ppermute | solution.py:14
  128.3 2.7 %collective-permute-done.14 = bf16[32,10,1,256]{3,0,2,1:T(8,128)(2,1)S(1)} collective-permute-done((bf16[32,10,1,256]{3,0,2,1:T(8,128)(2,1)S(1)}, bf16[32,10,1,256]{3,0,2,1:T(8,128)(2,1)S(1)}, u32[]{:S(2)}, u32[]{:S(2)}) %collective-permute-start.14) | collective-permute-done | bytes 163872 | tf_op jit(solution)/shard_map/ppermute | solution.py:13
  131.1 4.3 %collective-permute-done.15 = bf16[32,10,1,256]{3,0,2,1:T(8,128)(2,1)S(1)} collective-permute-done((bf16[32,10,1,256]{3,0,2,1:T(8,128)(2,1)S(1)}, bf16[32,10,1,256]{3,0,2,1:T(8,128)(2,1)S(1)}, u32[]{:S(2)}, u32[]{:S(2)}) %collective-permute-start.15) | collective-permute-done | bytes 163872 | tf_op jit(solution)/shard_map/ppermute | solution.py:14
  135.3 10.2 %maximum_convert_fusion = bf16[32,8,32,256]{3,0,2,1:T(8,128)(2,1)S(1)} fusion(bf16[32,10,1,256]{3,0,2,1:T(8,128)(2,1)S(1)} %collective-permute-done.15, bf16[32,1,32,256]{3,0,2,1:T(8,128)(2,1)S(1)} %collective-permute-done.13, bf16[32,8,32,256]{3,0,2,1:T(8,128)(2,1)S(1)} %maximum_convert_fusion.1, bf16[32,1,32,256]{3,0,2,1:T(8,128)(2,1)S(1)} %collective-permute-done.12, ...), kind=kOutput, calls=%fused_computation | convolution fusion | flops 9681108992 | bytes 10945536 | tf_op jit(solution)/shard_map/conv_general_dilated | solution.py:32
  145.6 4.4 %copy.7 = bf16[32,8,32,256]{3,2,1,0:T(8,128)(2,1)} copy(bf16[32,8,32,256]{3,0,2,1:T(8,128)(2,1)S(1)} %maximum_convert_fusion) | data formatting | bytes 8388608 | tf_op jit(solution)/shard_map/convert_element_type | solution.py:33
  (12 shorter events, 0.2 us)
Async XLA Ops:
  0.0 12.3 %copy-start = (bf16[32,8,32,256]{3,2,1,0:T(8,128)(2,1)S(1)}, bf16[32,8,32,256]{3,2,1,0:T(8,128)(2,1)}, u32[]{:S(2)}) copy-start(bf16[32,8,32,256]{3,2,1,0:T(8,128)(2,1)} %param.3) | copy-start | bytes 12582916
  1.7 10.5 %collective-permute-start = (bf16[32,1,32,256]{3,0,2,1:T(8,128)(2,1)S(1)}, bf16[32,1,32,256]{3,0,2,1:T(8,128)(2,1)S(1)}, u32[]{:S(2)}, u32[]{:S(2)}) collective-permute-start(bf16[32,1,32,256]{3,0,2,1:T(8,128)(2,1)S(1)} %copy.9), channel_id=1, source_target_pairs={{0,1},{1,2},{2,3},{3,4},{4,5},{5,6},{6,7},{8,9},{9,10},{10,11},{11... | collective-permute-start | bytes 1572872 | tf_op jit(solution)/shard_map/ppermute | solution.py:13
  4.0 11.0 %collective-permute-start.1 = (bf16[32,1,32,256]{3,0,2,1:T(8,128)(2,1)S(1)}, bf16[32,1,32,256]{3,0,2,1:T(8,128)(2,1)S(1)}, u32[]{:S(2)}, u32[]{:S(2)}) collective-permute-start(bf16[32,1,32,256]{3,0,2,1:T(8,128)(2,1)S(1)} %copy.10), channel_id=1, source_target_pairs={{1,0},{2,1},{3,2},{4,3},{5,4},{6,5},{7,6},{9,8},{10,9},{11,10},{12... | collective-permute-start | bytes 1572872 | tf_op jit(solution)/shard_map/ppermute | solution.py:14
  12.2 17.4 %slice-start = ((s8[4718592]{0:T(1024)(128)(4,1)}), s8[4194304]{0:T(1024)(128)(4,1)S(1)}, s32[]{:S(2)}) async-start(s8[4718592]{0:T(1024)(128)(4,1)} %bitcast.20), calls=%async_computation | async-start | bytes 8388608
  12.3 8.6 %copy-start.1 = (f32[4,256]{1,0:T(4,128)S(1)}, f32[4,256]{1,0:T(4,128)}, u32[]{:S(2)}) copy-start(f32[4,256]{1,0:T(4,128)} %param.5) | copy-start | bytes 12292
  12.3 17.3 %slice-start.1 = ((s8[4718592]{0:T(1024)(128)(4,1)}), s8[524288]{0:T(1024)(128)(4,1)S(1)}, s32[]{:S(2)}) async-start(s8[4718592]{0:T(1024)(128)(4,1)} %bitcast.20), calls=%async_computation.1 | async-start | bytes 1048576
  15.0 8.8 %collective-permute-start.2 = (bf16[32,10,1,256]{3,0,2,1:T(8,128)(2,1)S(1)}, bf16[32,10,1,256]{3,0,2,1:T(8,128)(2,1)S(1)}, u32[]{:S(2)}, u32[]{:S(2)}) collective-permute-start(bf16[32,10,1,256]{3,0,2,1:T(8,128)(2,1)S(1)} %get-tuple-element.11), channel_id=1, source_target_pairs={{0,8},{8,16},{16,24},{24,32},{32,40},{40,48},{48,56},{56,64},{64,7... | collective-permute-start | bytes 491528 | tf_op jit(solution)/shard_map/ppermute | solution.py:13
  18.5 11.1 %collective-permute-start.3 = (bf16[32,10,1,256]{3,0,2,1:T(8,128)(2,1)S(1)}, bf16[32,10,1,256]{3,0,2,1:T(8,128)(2,1)S(1)}, u32[]{:S(2)}, u32[]{:S(2)}) collective-permute-start(bf16[32,10,1,256]{3,0,2,1:T(8,128)(2,1)S(1)} %get-tuple-element.12), channel_id=1, source_target_pairs={{8,0},{16,8},{24,16},{32,24},{40,32},{48,40},{56,48},{64,56},{72,6... | collective-permute-start | bytes 491528 | tf_op jit(solution)/shard_map/ppermute | solution.py:14
  39.9 10.5 %collective-permute-start.4 = (bf16[32,1,32,256]{3,0,2,1:T(8,128)(2,1)S(1)}, bf16[32,1,32,256]{3,0,2,1:T(8,128)(2,1)S(1)}, u32[]{:S(2)}, u32[]{:S(2)}) collective-permute-start(bf16[32,1,32,256]{3,0,2,1:T(8,128)(2,1)S(1)} %get-tuple-element.17), channel_id=1, source_target_pairs={{0,1},{1,2},{2,3},{3,4},{4,5},{5,6},{6,7},{8,9},{9,10},{10,11},{11... | collective-permute-start | bytes 1572872 | tf_op jit(solution)/shard_map/ppermute | solution.py:13
  41.8 10.3 %collective-permute-start.5 = (bf16[32,1,32,256]{3,0,2,1:T(8,128)(2,1)S(1)}, bf16[32,1,32,256]{3,0,2,1:T(8,128)(2,1)S(1)}, u32[]{:S(2)}, u32[]{:S(2)}) collective-permute-start(bf16[32,1,32,256]{3,0,2,1:T(8,128)(2,1)S(1)} %get-tuple-element.18), channel_id=1, source_target_pairs={{1,0},{2,1},{3,2},{4,3},{5,4},{6,5},{7,6},{9,8},{10,9},{11,10},{12... | collective-permute-start | bytes 1572872 | tf_op jit(solution)/shard_map/ppermute | solution.py:14
  52.2 8.3 %collective-permute-start.6 = (bf16[32,10,1,256]{3,0,2,1:T(8,128)(2,1)S(1)}, bf16[32,10,1,256]{3,0,2,1:T(8,128)(2,1)S(1)}, u32[]{:S(2)}, u32[]{:S(2)}) collective-permute-start(bf16[32,10,1,256]{3,0,2,1:T(8,128)(2,1)S(1)} %get-tuple-element.9), channel_id=1, source_target_pairs={{0,8},{8,16},{16,24},{24,32},{32,40},{40,48},{48,56},{56,64},{64,7... | collective-permute-start | bytes 491528 | tf_op jit(solution)/shard_map/ppermute | solution.py:13
  54.1 10.4 %collective-permute-start.7 = (bf16[32,10,1,256]{3,0,2,1:T(8,128)(2,1)S(1)}, bf16[32,10,1,256]{3,0,2,1:T(8,128)(2,1)S(1)}, u32[]{:S(2)}, u32[]{:S(2)}) collective-permute-start(bf16[32,10,1,256]{3,0,2,1:T(8,128)(2,1)S(1)} %get-tuple-element.10), channel_id=1, source_target_pairs={{8,0},{16,8},{24,16},{32,24},{40,32},{48,40},{56,48},{64,56},{72,6... | collective-permute-start | bytes 491528 | tf_op jit(solution)/shard_map/ppermute | solution.py:14
  74.9 10.5 %collective-permute-start.8 = (bf16[32,1,32,256]{3,0,2,1:T(8,128)(2,1)S(1)}, bf16[32,1,32,256]{3,0,2,1:T(8,128)(2,1)S(1)}, u32[]{:S(2)}, u32[]{:S(2)}) collective-permute-start(bf16[32,1,32,256]{3,0,2,1:T(8,128)(2,1)S(1)} %get-tuple-element.15), channel_id=1, source_target_pairs={{0,1},{1,2},{2,3},{3,4},{4,5},{5,6},{6,7},{8,9},{9,10},{10,11},{11... | collective-permute-start | bytes 1572872 | tf_op jit(solution)/shard_map/ppermute | solution.py:13
  77.5 9.6 %collective-permute-start.9 = (bf16[32,1,32,256]{3,0,2,1:T(8,128)(2,1)S(1)}, bf16[32,1,32,256]{3,0,2,1:T(8,128)(2,1)S(1)}, u32[]{:S(2)}, u32[]{:S(2)}) collective-permute-start(bf16[32,1,32,256]{3,0,2,1:T(8,128)(2,1)S(1)} %get-tuple-element.16), channel_id=1, source_target_pairs={{1,0},{2,1},{3,2},{4,3},{5,4},{6,5},{7,6},{9,8},{10,9},{11,10},{12... | collective-permute-start | bytes 1572872 | tf_op jit(solution)/shard_map/ppermute | solution.py:14
  87.2 8.4 %collective-permute-start.10 = (bf16[32,10,1,256]{3,0,2,1:T(8,128)(2,1)S(1)}, bf16[32,10,1,256]{3,0,2,1:T(8,128)(2,1)S(1)}, u32[]{:S(2)}, u32[]{:S(2)}) collective-permute-start(bf16[32,10,1,256]{3,0,2,1:T(8,128)(2,1)S(1)} %get-tuple-element.7), channel_id=1, source_target_pairs={{0,8},{8,16},{16,24},{24,32},{32,40},{40,48},{48,56},{56,64},{64,7... | collective-permute-start | bytes 491528 | tf_op jit(solution)/shard_map/ppermute | solution.py:13
  89.1 10.5 %collective-permute-start.11 = (bf16[32,10,1,256]{3,0,2,1:T(8,128)(2,1)S(1)}, bf16[32,10,1,256]{3,0,2,1:T(8,128)(2,1)S(1)}, u32[]{:S(2)}, u32[]{:S(2)}) collective-permute-start(bf16[32,10,1,256]{3,0,2,1:T(8,128)(2,1)S(1)} %get-tuple-element.8), channel_id=1, source_target_pairs={{8,0},{16,8},{24,16},{32,24},{40,32},{48,40},{56,48},{64,56},{72,6... | collective-permute-start | bytes 491528 | tf_op jit(solution)/shard_map/ppermute | solution.py:14
  110.0 10.5 %collective-permute-start.12 = (bf16[32,1,32,256]{3,0,2,1:T(8,128)(2,1)S(1)}, bf16[32,1,32,256]{3,0,2,1:T(8,128)(2,1)S(1)}, u32[]{:S(2)}, u32[]{:S(2)}) collective-permute-start(bf16[32,1,32,256]{3,0,2,1:T(8,128)(2,1)S(1)} %get-tuple-element.13), channel_id=1, source_target_pairs={{0,1},{1,2},{2,3},{3,4},{4,5},{5,6},{6,7},{8,9},{9,10},{10,11},{11... | collective-permute-start | bytes 1572872 | tf_op jit(solution)/shard_map/ppermute | solution.py:13
  112.5 9.7 %collective-permute-start.13 = (bf16[32,1,32,256]{3,0,2,1:T(8,128)(2,1)S(1)}, bf16[32,1,32,256]{3,0,2,1:T(8,128)(2,1)S(1)}, u32[]{:S(2)}, u32[]{:S(2)}) collective-permute-start(bf16[32,1,32,256]{3,0,2,1:T(8,128)(2,1)S(1)} %get-tuple-element.14), channel_id=1, source_target_pairs={{1,0},{2,1},{3,2},{4,3},{5,4},{6,5},{7,6},{9,8},{10,9},{11,10},{12... | collective-permute-start | bytes 1572872 | tf_op jit(solution)/shard_map/ppermute | solution.py:14
  122.2 8.8 %collective-permute-start.14 = (bf16[32,10,1,256]{3,0,2,1:T(8,128)(2,1)S(1)}, bf16[32,10,1,256]{3,0,2,1:T(8,128)(2,1)S(1)}, u32[]{:S(2)}, u32[]{:S(2)}) collective-permute-start(bf16[32,10,1,256]{3,0,2,1:T(8,128)(2,1)S(1)} %get-tuple-element.5), channel_id=1, source_target_pairs={{0,8},{8,16},{16,24},{24,32},{32,40},{40,48},{48,56},{56,64},{64,7... | collective-permute-start | bytes 491528 | tf_op jit(solution)/shard_map/ppermute | solution.py:13
  124.4 11.0 %collective-permute-start.15 = (bf16[32,10,1,256]{3,0,2,1:T(8,128)(2,1)S(1)}, bf16[32,10,1,256]{3,0,2,1:T(8,128)(2,1)S(1)}, u32[]{:S(2)}, u32[]{:S(2)}) collective-permute-start(bf16[32,10,1,256]{3,0,2,1:T(8,128)(2,1)S(1)} %get-tuple-element.6), channel_id=1, source_target_pairs={{8,0},{16,8},{24,16},{32,24},{40,32},{48,40},{56,48},{64,56},{72,6... | collective-permute-start | bytes 491528 | tf_op jit(solution)/shard_map/ppermute | solution.py:14
where the time goes:
time: 151 us; the launch traced here: 150 us
  waiting for transfers between devices  53.2 us (35%)
  starting transfers between devices  46 us (30%)
  matrix products  41 us (27%)
  local copies, waits for them, and re-layouts  9.38 us (6%)
    conv_general_dilated x4, matrix products, local_stack(): lax.conv_general_dilated(padded, weights[layer_idx], (1, 1), 'VALID', dim...  41 us
    ppermute x8, waiting for transfers between devices, edge_exchange(): from_prev = lax.ppermute(tail_edge, axis_name, perm=to_next)  29.9 us
    ppermute x8, starting transfers between devices, edge_exchange(): from_next = lax.ppermute(head_edge, axis_name, perm=to_prev)  27.5 us
    ppermute x8, waiting for transfers between devices, edge_exchange(): from_next = lax.ppermute(head_edge, axis_name, perm=to_prev)  23.3 us
    ppermute x8, starting transfers between devices, edge_exchange(): from_prev = lax.ppermute(tail_edge, axis_name, perm=to_next)  18.5 us
    convert_element_type x1, local copies, waits for them, and re-layouts, local_stack(): hidden = jnp.maximum(summed + biases[layer_idx], 0.0).astype(jnp.bfloat16)  4.43 us
    unnamed x12, local copies, waits for them, and re-layouts  3.25 us
  transfers between devices with their start and end apart: 16, of which 15 were waited for; matrix products, arithmetic and copies ran while one was open for 2% of the time, Pallas kernels for 0%

commit v1 on v0

v1 whole, which is shorter than its diff:
```python
import functools

import jax
import jax.numpy as jnp
from jax import lax
from jax.experimental import pallas as pl
from jax.experimental.pallas import tpu as pltpu
from jax.sharding import PartitionSpec as P

MESH = pl.DeviceIdType.MESH
LANES = 128
GROUPS = 2
ROW_ORDER = (0, 7, 1, 2, 3, 4, 5, 6)


def kernel(dims, x_hbm, w_hbm, b_ref, o_hbm, act, w_vm, in_sem, out_sem, send_sem, recv_sem):
    layers, imgs, rows, cols, ch, row_devs, col_devs = dims
    halves = ch // LANES
    taps = 9
    row, col = lax.axis_index("row"), lax.axis_index("col")
    has = {(-1, 0): row > 0, (1, 0): row < row_devs - 1, (0, -1): col > 0, (0, 1): col < col_devs - 1}

    def exists(dr, dc):
        if dr and dc:
            return jnp.logical_and(has[(dr, 0)], has[(0, dc)])
        return has[(dr, dc)]

    def span(step, size):
        if step < 0:
            return pl.ds(1, 1), pl.ds(size + 1, 1)
        if step > 0:
            return pl.ds(size, 1), pl.ds(0, 1)
        return pl.ds(1, size), pl.ds(1, size)

    nbrs = [(-1, 0), (1, 0), (0, -1), (0, 1), (-1, -1), (-1, 1), (1, -1), (1, 1)]

    def edge_copy(buf, n):
        dr, dc = nbrs[n]
        src_r, dst_r = span(dr, rows)
        src_c, dst_c = span(dc, cols)
        return pltpu.make_async_remote_copy(
            src_ref=act.at[buf, src_r, src_c],
            dst_ref=act.at[buf, dst_r, dst_c],
            send_sem=send_sem.at[buf, n],
            recv_sem=recv_sem.at[buf, n],
            device_id={"row": row + dr, "col": col + dc},
            device_id_type=MESH,
        )

    def send(buf, which):
        for n in which:
            @pl.when(exists(*nbrs[n]))
            def _(n=n):
                edge_copy(buf, n).start()

    w_copies = []
    for l in range(layers):
        for hf in range(halves):
            w_copies.append(pltpu.make_async_copy(
                w_hbm.at[l, :, pl.ds(hf * LANES, LANES)],
                w_vm.at[l, hf], in_sem.at[GROUPS + l * halves + hf]))
    x_copies = [pltpu.make_async_copy(x_hbm.at[g], act.at[g, pl.ds(1, rows), pl.ds(1, cols)], in_sem.at[g]) for g in range(GROUPS)]
    for c in x_copies:
        c.start()
    for c in w_copies:
        c.start()

    barrier = pltpu.get_barrier_semaphore()
    for n, (dr, dc) in enumerate(nbrs):
        @pl.when(exists(dr, dc))
        def _(dr=dr, dc=dc):
            pl.semaphore_signal(barrier, inc=1, device_id={"row": row + dr, "col": col + dc}, device_id_type=MESH)
    n_row = 1 + sum(has[(d, 0)].astype(jnp.int32) for d in (-1, 1))
    n_col = 1 + sum(has[(0, d)].astype(jnp.int32) for d in (-1, 1))
    pl.semaphore_wait(barrier, n_row * n_col - 1)

    for g in range(GROUPS):
        x_copies[g].wait()
        send(g, range(8))

    def zero_borders(buf, carry):
        @pl.when(row == 0)
        def _():
            act[buf, 0] = jnp.zeros(act.shape[2:], act.dtype)

        @pl.when(row == row_devs - 1)
        def _():
            act[buf, rows + 1] = jnp.zeros(act.shape[2:], act.dtype)

        @pl.when(col == 0)
        def _():
            act[buf, :, 0] = jnp.zeros((rows + 2,) + act.shape[3:], act.dtype)

        @pl.when(col == col_devs - 1)
        def _():
            act[buf, :, cols + 1] = jnp.zeros((rows + 2,) + act.shape[3:], act.dtype)
        return carry

    lax.fori_loop(0, layers * GROUPS, zero_borders, 0)
    for c in w_copies:
        c.wait()

    def row_out(p, buf, layer, r):
        pieces = []
        for t in range(taps):
            tap = act[p, r + t // 3, pl.ds(t % 3, cols)]
            pieces += [tap[:, hf].reshape(cols * imgs, LANES) for hf in range(halves)]
        lhs = jnp.concatenate(pieces, axis=1)
        wt = jnp.concatenate([w_vm[layer, hf] for hf in range(halves)], axis=1)
        y = jnp.dot(lhs, wt, preferred_element_type=jnp.float32)
        y = jnp.maximum(y + b_ref[layer], 0.0).astype(jnp.bfloat16)
        for hf in range(halves):
            act[buf, r + 1, pl.ds(1, cols), hf] = y[:, hf * LANES:(hf + 1) * LANES].reshape(cols, imgs, LANES)

    def phase(p, carry):
        layer = p // GROUPS
        for n in range(8):
            @pl.when(exists(-nbrs[n][0], -nbrs[n][1]))
            def _(n=n):
                edge_copy(p, n).wait_recv()

        for i, r in enumerate(ROW_ORDER):
            row_out(p, p + GROUPS, layer, r)
            if i == 3:
                @pl.when(p < (layers - 1) * GROUPS)
                def _():
                    send(p + GROUPS, (0, 1, 4, 5, 6, 7))
        @pl.when(p < (layers - 1) * GROUPS)
        def _():
            send(p + GROUPS, (2, 3))
        return carry

    lax.fori_loop(0, layers * GROUPS, phase, 0)

    out_copies = [pltpu.make_async_copy(act.at[layers * GROUPS + g, pl.ds(1, rows), pl.ds(1, cols)], o_hbm.at[g], out_sem.at[g]) for g in range(GROUPS)]
    for c in out_copies:
        c.start()

    def finish(buf, carry):
        for n in range(8):
            @pl.when(exists(*nbrs[n]))
            def _(n=n):
                edge_copy(buf, n).wait_send()
        return carry

    lax.fori_loop(0, layers * GROUPS, finish, 0)
    for c in out_copies:
        c.wait()


def solution(mesh):
    row_devs = mesh.shape["row"]
    col_devs = mesh.shape["col"]
    act_spec = P("ens", "row", "col", None)

    def local_stack(x_tile, weights, biases):
        batch, rows, cols, ch = x_tile.shape
        layers = weights.shape[0]
        imgs = batch // GROUPS
        halves = ch // LANES
        dims = (layers, imgs, rows, cols, ch, row_devs, col_devs)
        x = x_tile.reshape(GROUPS, imgs, rows, cols, halves, LANES).transpose(0, 2, 3, 4, 1, 5)
        w = weights.reshape(layers, 9 * ch, ch)
        b = biases.reshape(layers, 1, ch)
        any_spec = pl.BlockSpec(memory_space=pl.ANY)
        y = pl.pallas_call(
            functools.partial(kernel, dims),
            out_shape=jax.ShapeDtypeStruct((GROUPS, rows, cols, halves, imgs, LANES), jnp.bfloat16),
            in_specs=[any_spec, any_spec, pl.BlockSpec(memory_space=pltpu.VMEM)],
            out_specs=any_spec,
            scratch_shapes=[
                pltpu.VMEM(((layers + 1) * GROUPS, rows + 2, cols + 2, halves, imgs, LANES), jnp.bfloat16),
                pltpu.VMEM((layers, halves, 9 * ch, LANES), jnp.bfloat16),
                pltpu.SemaphoreType.DMA((GROUPS + layers * halves,)),
                pltpu.SemaphoreType.DMA((GROUPS,)),
                pltpu.SemaphoreType.DMA((layers * GROUPS, 8)),
                pltpu.SemaphoreType.DMA((layers * GROUPS, 8)),
            ],
            compiler_params=pltpu.CompilerParams(collective_id=0, has_side_effects=True, vmem_limit_bytes=48 * 1024 * 1024),
            name="conv_stack",
        )(x, w, b)
        return y.transpose(0, 4, 1, 2, 3, 5).reshape(batch, rows, cols, ch)

    return jax.shard_map(local_stack, mesh=mesh, in_specs=(act_spec, P(), P()), out_specs=act_spec, check_vma=False)
```

time: 151 us -> 86.5 us (0.57)
  the two profiles are of different devices: /device:TPU:26 before, /device:TPU:97 now
where the time goes in v1:
time: 86.5 us; the launch traced here: 86.1 us
  Pallas kernels  53.4 us (62%)
  local copies, waits for them, and re-layouts  32.7 us (38%)
    pallas_call x1, Pallas kernels, local_stack(): pl.pallas_call(functools.partial(kernel, dims), out_shape=jax.ShapeDtypeS...  53.4 us
    reshape x2, local copies, waits for them, and re-layouts, local_stack(): x_tile.reshape(GROUPS, imgs, rows, cols, halves, LANES)  17.6 us
    reshape x1, local copies, waits for them, and re-layouts, local_stack(): return y.transpose(0, 4, 1, 2, 3, 5).reshape(batch, rows, cols, ch)  7.58 us
    transpose x1, local copies, waits for them, and re-layouts, local_stack(): return y.transpose(0, 4, 1, 2, 3, 5).reshape(batch, rows, cols, ch)  6.76 us

profile of v1, /device:TPU:97, one launch (start us, length us, event | category | flops | bytes accessed | tf_op | source)
XLA Modules:
  0.0 86.1 jit_solution(9823241789889664997)
XLA Ops:
  0.0 0.7 reshape.14.b_ref
  0.7 6.9 %reshape.12 = bf16[2,16,8,32,2,128]{5,4,3,2,1,0:T(2,128)(2,1)} reshape(bf16[32,8,32,256]{3,2,1,0:T(8,128)(2,1)} %param.3) | data formatting | bytes 8388608 | tf_op jit(solution)/shard_map/reshape | solution.py:162
  7.6 10.7 %copy.7 = bf16[2,16,8,32,2,128]{5,1,4,3,2,0:T(8,128)(2,1)} copy(bf16[2,16,8,32,2,128]{5,4,3,2,1,0:T(2,128)(2,1)} %reshape.12) | data formatting | bytes 8388608 | tf_op jit(solution)/shard_map/reshape | solution.py:162
  18.3 53.4 %conv_stack.1 = bf16[2,8,32,2,16,128]{5,4,3,2,1,0:T(8,128)(2,1)S(1)} custom-call(bf16[2,8,32,2,16,128]{5,4,3,2,1,0:T(8,128)(2,1)} %bitcast.8, bf16[4,2304,256]{2,1,0:T(8,128)(2,1)} %bitcast.9, f32[4,1,256]{2,1,0:T(1,128)S(1)} %reshape.14.b_ref), custom_call_target="tpu_custom_call" | custom-call | tf_op jit(solution)/shard_map/conv_stack/pallas_call | solution.py:166
  71.7 6.8 %copy.5 = bf16[2,16,8,32,2,128]{5,4,3,2,1,0:T(2,128)(2,1)} copy(bf16[2,16,8,32,2,128]{5,1,4,3,2,0:T(8,128)(2,1)S(1)} %bitcast.7) | data formatting | bytes 8388608 | tf_op jit(solution)/shard_map/transpose | solution.py:182
  78.5 7.6 %reshape.15 = bf16[32,8,32,256]{3,2,1,0:T(8,128)(2,1)} reshape(bf16[2,16,8,32,2,128]{5,4,3,2,1,0:T(2,128)(2,1)} %copy.5) | data formatting | bytes 8388608 | tf_op jit(solution)/shard_map/reshape | solution.py:182

commit v2 on v1

v2 whole, which is shorter than its diff:
```python
import functools

import jax
import jax.numpy as jnp
from jax import lax
from jax.experimental import pallas as pl
from jax.experimental.pallas import tpu as pltpu
from jax.sharding import PartitionSpec as P

MESH = pl.DeviceIdType.MESH
LANES = 128
GROUPS = 2
TAPS = 9
NBRS = ((-1, 0), (1, 0), (0, -1), (0, 1), (-1, -1), (-1, 1), (1, -1), (1, 1))
ROW_SENDS = (0, 1, 4, 5, 6, 7)
COL_SENDS = (2, 3)


def kernel(dims, x_hbm, w_hbm, b_hbm, o_ref, act, w_vm, b_ref, x_vm, perm, turn, in_sem, send_sem, recv_sem):
    layers, imgs, rows, cols, ch, row_devs, col_devs = dims
    halves = ch // LANES
    pitch = cols + 8
    row, col = lax.axis_index("row"), lax.axis_index("col")
    has = {(-1, 0): row > 0, (1, 0): row < row_devs - 1, (0, -1): col > 0, (0, 1): col < col_devs - 1}

    def exists(dr, dc):
        if dr and dc:
            return jnp.logical_and(has[(dr, 0)], has[(0, dc)])
        return has[(dr, dc)]

    def span(step, size):
        if step < 0:
            return pl.ds(1, 1), pl.ds(size + 1, 1)
        if step > 0:
            return pl.ds(size, 1), pl.ds(0, 1)
        return pl.ds(1, size), pl.ds(1, size)

    def edge_copy(buf, n):
        dr, dc = NBRS[n]
        src_r, dst_r = span(dr, rows)
        src_c, dst_c = span(dc, cols)
        return pltpu.make_async_remote_copy(
            src_ref=act.at[buf, src_r, src_c],
            dst_ref=act.at[buf, dst_r, dst_c],
            send_sem=send_sem.at[buf, n],
            recv_sem=recv_sem.at[buf, n],
            device_id={"row": row + dr, "col": col + dc},
            device_id_type=MESH,
        )

    def send(buf, which):
        for n in which:
            @pl.when(exists(*NBRS[n]))
            def _(n=n):
                edge_copy(buf, n).start()

    def receive(buf):
        for n, (dr, dc) in enumerate(NBRS):
            @pl.when(exists(-dr, -dc))
            def _(n=n):
                edge_copy(buf, n).wait_recv()

    x_copies, w_copies = [], []
    for g in range(GROUPS):
        for hf in range(halves):
            x_copies.append(pltpu.make_async_copy(
                x_hbm.at[pl.ds(g * imgs, imgs), :, :, pl.ds(hf * LANES, LANES)], x_vm.at[g, hf], in_sem.at[g * halves + hf]))
    for l in range(layers):
        for hf in range(halves):
            w_copies.append(pltpu.make_async_copy(
                w_hbm.at[l, :, pl.ds(hf * LANES, LANES)], w_vm.at[l, hf], in_sem.at[(GROUPS + l) * halves + hf]))
    b_copy = pltpu.make_async_copy(b_hbm, b_ref, in_sem.at[(GROUPS + layers) * halves])
    for c in x_copies + w_copies + [b_copy]:
        c.start()

    barrier = pltpu.get_barrier_semaphore()
    for dr, dc in NBRS:
        @pl.when(exists(dr, dc))
        def _(dr=dr, dc=dc):
            pl.semaphore_signal(barrier, inc=1, device_id={"row": row + dr, "col": col + dc}, device_id_type=MESH)

    def zero_borders(buf, carry):
        @pl.when(row == 0)
        def _():
            act[buf, 0] = jnp.zeros(act.shape[2:], act.dtype)

        @pl.when(row == row_devs - 1)
        def _():
            act[buf, rows + 1] = jnp.zeros(act.shape[2:], act.dtype)

        @pl.when(col == 0)
        def _():
            act[buf, :, 0] = jnp.zeros((rows + 2,) + act.shape[3:], act.dtype)

        @pl.when(col == col_devs - 1)
        def _():
            act[buf, :, cols + 1] = jnp.zeros((rows + 2,) + act.shape[3:], act.dtype)
        return carry

    lax.fori_loop(0, layers * GROUPS, zero_borders, 0)

    block = imgs * imgs
    out_row = lax.broadcasted_iota(jnp.int32, (block, block), 0)
    in_row = lax.broadcasted_iota(jnp.int32, (block, block), 1)
    swapped = (out_row % imgs) * imgs + out_row // imgs
    perm[...] = jnp.where(in_row == swapped, 1.0, 0.0).astype(jnp.bfloat16)

    n_row = 1 + sum(has[(d, 0)].astype(jnp.int32) for d in (-1, 1))
    n_col = 1 + sum(has[(0, d)].astype(jnp.int32) for d in (-1, 1))
    pl.semaphore_wait(barrier, n_row * n_col - 1)

    def put(buf, r, first, count, y):
        for hf in range(halves):
            act[buf, r + 1, pl.ds(first + 1, count), hf] = y[:, hf * LANES:(hf + 1) * LANES].reshape(count, imgs, LANES)

    order = (0, rows - 1) + tuple(range(1, rows - 1))
    for g in range(GROUPS):
        for hf in range(halves):
            x_copies[g * halves + hf].wait()
        for i, r in enumerate(order):
            for first in range(0, cols, imgs):
                tile = jnp.concatenate([x_vm[g, hf, :, r, pl.ds(first, imgs)].reshape(block, LANES) for hf in range(halves)], axis=1)
                y = jnp.dot(perm[...], tile, preferred_element_type=jnp.float32)
                put(g, r, first, imgs, y.astype(jnp.bfloat16))
            if i == 2:
                send(g, ROW_SENDS)
        send(g, COL_SENDS)
    for c in w_copies + [b_copy]:
        c.wait()

    def conv(taps, layer):
        lhs = jnp.concatenate([tap[..., hf, :, :].reshape(-1, LANES) for tap in taps for hf in range(halves)], axis=1)
        wt = jnp.concatenate([w_vm[layer, hf] for hf in range(halves)], axis=1)
        y = jnp.dot(lhs, wt, preferred_element_type=jnp.float32)
        return jnp.maximum(y + b_ref[pl.ds(layer, 1), :], 0.0)

    def conv_row(p, layer, r, first, count):
        return conv([act[p, r + t // 3, pl.ds(first + t % 3, count)] for t in range(TAPS)], layer)

    def first_layer(g, carry):
        for r in range(1, rows - 1):
            y = conv_row(g, 0, r, 1, cols - 2)
            put(g + GROUPS, r, 1, cols - 2, y.astype(jnp.bfloat16))
        receive(g)
        for r in (0, rows - 1):
            y = conv_row(g, 0, r, 0, cols)
            put(g + GROUPS, r, 0, cols, y.astype(jnp.bfloat16))
        taps = []
        for t in range(TAPS):
            sides = [act[g, pl.ds(1 + t // 3, rows - 2), c + t % 3] for c in (0, cols - 1)]
            taps.append(jnp.concatenate(sides, axis=0))
        y = conv(taps, 0).astype(jnp.bfloat16)
        half = (rows - 2) * imgs
        for s, c in enumerate((0, cols - 1)):
            for hf in range(halves):
                piece = y[s * half:(s + 1) * half, hf * LANES:(hf + 1) * LANES]
                act[g + GROUPS, pl.ds(2, rows - 2), c + 1, hf] = piece.reshape(rows - 2, imgs, LANES)
        send(g + GROUPS, ROW_SENDS + COL_SENDS)
        return carry

    lax.fori_loop(0, GROUPS, first_layer, 0)

    def middle_layer(p, carry):
        receive(p)
        for i, r in enumerate(order):
            y = conv_row(p, p // GROUPS, r, 0, cols)
            put(p + GROUPS, r, 0, cols, y.astype(jnp.bfloat16))
            if i == 2:
                send(p + GROUPS, ROW_SENDS)
        send(p + GROUPS, COL_SENDS)
        return carry

    lax.fori_loop(GROUPS, (layers - 1) * GROUPS, middle_layer, 0)

    def last_layer(g, carry):
        p = (layers - 1) * GROUPS + g
        receive(p)
        for r in range(rows):
            y = conv_row(p, layers - 1, r, 0, cols)
            for c in range(cols):
                for hf in range(halves):
                    turn[r % 2, hf, pl.ds(c, imgs, stride=pitch), :] = y[c * imgs:(c + 1) * imgs, hf * LANES:(hf + 1) * LANES]
            for i in range(imgs):
                for hf in range(halves):
                    line = turn[r % 2, hf, pl.ds(i * pitch, cols), :].astype(jnp.bfloat16)
                    o_ref[g * imgs + i, r, :, pl.ds(hf * LANES, LANES)] = line
        return carry

    lax.fori_loop(0, GROUPS, last_layer, 0)

    def finish(buf, carry):
        for n in range(len(NBRS)):
            @pl.when(exists(*NBRS[n]))
            def _(n=n):
                edge_copy(buf, n).wait_send()
        return carry

    lax.fori_loop(0, layers * GROUPS, finish, 0)


def solution(mesh):
    row_devs = mesh.shape["row"]
    col_devs = mesh.shape["col"]
    act_spec = P("ens", "row", "col", None)

    def local_stack(x_tile, weights, biases):
        batch, rows, cols, ch = x_tile.shape
        layers = weights.shape[0]
        imgs = batch // GROUPS
        halves = ch // LANES
        dims = (layers, imgs, rows, cols, ch, row_devs, col_devs)
        hbm = pl.BlockSpec(memory_space=pltpu.HBM)
        return pl.pallas_call(
            functools.partial(kernel, dims),
            out_shape=pltpu.VMEM((batch, rows, cols, ch), jnp.bfloat16),
            in_specs=[hbm, hbm, hbm],
            out_specs=pl.BlockSpec(memory_space=pltpu.VMEM),
            scratch_shapes=[
                pltpu.VMEM((layers * GROUPS, rows + 2, cols + 2, halves, imgs, LANES), jnp.bfloat16),
                pltpu.VMEM((layers, halves, TAPS * ch, LANES), jnp.bfloat16),
                pltpu.VMEM((layers, ch), jnp.float32),
                pltpu.VMEM((GROUPS, halves, imgs, rows, cols, LANES), jnp.bfloat16),
                pltpu.VMEM((imgs * imgs, imgs * imgs), jnp.bfloat16),
                pltpu.VMEM((2, halves, imgs * (cols + 8), LANES), jnp.float32),
                pltpu.SemaphoreType.DMA(((GROUPS + layers) * halves + 1,)),
                pltpu.SemaphoreType.DMA((layers * GROUPS, len(NBRS))),
                pltpu.SemaphoreType.DMA((layers * GROUPS, len(NBRS))),
            ],
            compiler_params=pltpu.CompilerParams(collective_id=0, has_side_effects=True, vmem_limit_bytes=56 * 1024 * 1024),
            name="conv_stack",
        )(x_tile, weights.reshape(layers, TAPS * ch, ch), biases)

    return jax.shard_map(local_stack, mesh=mesh, in_specs=(act_spec, P(), P()), out_specs=act_spec, check_vma=False)
```

time: 86.5 us -> 60.7 us (0.70)
  local copies, waits for them, and re-layouts: 32.7 us -> 2.02 us
  Pallas kernels: 53.4 us -> 58.5 us
    reshape x4 -> x0, local copies, waits for them, and re-layouts: 25.9 us -> none  [the longest x2 17.6 us: local_stack(): x_tile.reshape(GROUPS, imgs, rows, cols, halves, LANES)]
    transpose x1 -> x0, local copies, waits for them, and re-layouts: 6.76 us -> none  [local_stack(): return y.transpose(0, 4, 1, 2, 3, 5).reshape(batch, rows, cols, ch)]
    pallas_call x1, Pallas kernels: 53.4 us -> 58.5 us  [local_stack(): pl.pallas_call(functools.partial(kernel, dims), out_shape=pltpu.VMEM((bat...]
    unnamed x0 -> x1, local copies, waits for them, and re-layouts: none -> 2.02 us
where the time goes in v2:
time: 60.7 us; the launch traced here: 60.6 us
  Pallas kernels  58.5 us (96%)
  local copies, waits for them, and re-layouts  2.02 us (3%)
    pallas_call x1, Pallas kernels, local_stack(): pl.pallas_call(functools.partial(kernel, dims), out_shape=pltpu.VMEM((bat...  58.5 us
    unnamed x1, local copies, waits for them, and re-layouts  2.02 us

profile of v2, /device:TPU:97, one launch (start us, length us, event | category | flops | bytes accessed | tf_op | source)
XLA Modules:
  0.0 60.6 jit_solution(9888718107413749181)
XLA Ops:
  0.0 58.5 %conv_stack.1 = bf16[32,8,32,256]{3,2,1,0:T(8,128)(2,1)S(1)} custom-call(bf16[32,8,32,256]{3,2,1,0:T(8,128)(2,1)} %x_hbm.1, bf16[4,2304,256]{2,1,0:T(8,128)(2,1)} %bitcast.1, f32[4,256]{1,0:T(4,128)} %b_hbm.1), custom_call_target="tpu_custom_call" | custom-call | tf_op jit(solution)/shard_map/conv_stack/pallas_call | solution.py:213
  58.5 2.0 %copy.5 = bf16[32,8,32,256]{3,2,1,0:T(8,128)(2,1)} copy(bf16[32,8,32,256]{3,2,1,0:T(8,128)(2,1)S(1)} %conv_stack.1) | data formatting | bytes 8388608

commit v3 on v2

--- a/solution.py
+++ b/solution.py
@@ -21,44 +21,41 @@
     halves = ch // LANES
     pitch = cols + 8
     row, col = lax.axis_index("row"), lax.axis_index("col")
-    has = {(-1, 0): row > 0, (1, 0): row < row_devs - 1, (0, -1): col > 0, (0, 1): col < col_devs - 1}
-
-    def exists(dr, dc):
-        if dr and dc:
-            return jnp.logical_and(has[(dr, 0)], has[(0, dc)])
-        return has[(dr, dc)]
-
-    def span(step, size):
+
+    def span(step, size, at, devs):
         if step < 0:
-            return pl.ds(1, 1), pl.ds(size + 1, 1)
+            return pl.ds(1, 1), pl.ds(jnp.where(at == 0, size + 2, size + 1), 1), lax.rem(at + devs - 1, devs)
         if step > 0:
-            return pl.ds(size, 1), pl.ds(0, 1)
-        return pl.ds(1, size), pl.ds(1, size)
+            return pl.ds(size, 1), pl.ds(jnp.where(at == devs - 1, size + 2, 0), 1), lax.rem(at + 1, devs)
+        return pl.ds(1, size), pl.ds(1, size), at
+
+    spans = {}
+    for step in (-1, 0, 1):
+        spans["row", step] = span(step, rows, row, row_devs)
+        spans["col", step] = span(step, cols, col, col_devs)
+
+    def neighbour(n):
+        return {"row": spans["row", NBRS[n][0]][2], "col": spans["col", NBRS[n][1]][2]}
 
     def edge_copy(buf, n):
-        dr, dc = NBRS[n]
-        src_r, dst_r = span(dr, rows)
-        src_c, dst_c = span(dc, cols)
+        src_r, dst_r, _ = spans["row", NBRS[n][0]]
+        src_c, dst_c, _ = spans["col", NBRS[n][1]]
         return pltpu.make_async_remote_copy(
             src_ref=act.at[buf, src_r, src_c],
             dst_ref=act.at[buf, dst_r, dst_c],
             send_sem=send_sem.at[buf, n],
             recv_sem=recv_sem.at[buf, n],
-            device_id={"row": row + dr, "col": col + dc},
+            device_id=neighbour(n),
             device_id_type=MESH,
         )
 
     def send(buf, which):
         for n in which:
-            @pl.when(exists(*NBRS[n]))
-            def _(n=n):
-                edge_copy(buf, n).start()
+            edge_copy(buf, n).start()
 
     def receive(buf):
-        for n, (dr, dc) in enumerate(NBRS):
-            @pl.when(exists(-dr, -dc))
-            def _(n=n):
-                edge_copy(buf, n).wait_recv()
+        for n in range(len(NBRS)):
+            edge_copy(buf, n).wait_recv()
 
     x_copies, w_copies = [], []
     for g in range(GROUPS):
@@ -74,10 +71,8 @@
         c.start()
 
     barrier = pltpu.get_barrier_semaphore()
-    for dr, dc in NBRS:
-        @pl.when(exists(dr, dc))
-        def _(dr=dr, dc=dc):
-            pl.semaphore_signal(barrier, inc=1, device_id={"row": row + dr, "col": col + dc}, device_id_type=MESH)
+    for n in range(len(NBRS)):
+        pl.semaphore_signal(barrier, inc=1, device_id=neighbour(n), device_id_type=MESH)
 
     def zero_borders(buf, carry):
         @pl.when(row == 0)
@@ -90,11 +85,11 @@
 
         @pl.when(col == 0)
         def _():
-            act[buf, :, 0] = jnp.zeros((rows + 2,) + act.shape[3:], act.dtype)
+            act[buf, pl.ds(0, rows + 2), 0] = jnp.zeros((rows + 2,) + act.shape[3:], act.dtype)
 
         @pl.when(col == col_devs - 1)
         def _():
-            act[buf, :, cols + 1] = jnp.zeros((rows + 2,) + act.shape[3:], act.dtype)
+            act[buf, pl.ds(0, rows + 2), cols + 1] = jnp.zeros((rows + 2,) + act.shape[3:], act.dtype)
         return carry
 
     lax.fori_loop(0, layers * GROUPS, zero_borders, 0)
@@ -105,9 +100,7 @@
     swapped = (out_row % imgs) * imgs + out_row // imgs
     perm[...] = jnp.where(in_row == swapped, 1.0, 0.0).astype(jnp.bfloat16)
 
-    n_row = 1 + sum(has[(d, 0)].astype(jnp.int32) for d in (-1, 1))
-    n_col = 1 + sum(has[(0, d)].astype(jnp.int32) for d in (-1, 1))
-    pl.semaphore_wait(barrier, n_row * n_col - 1)
+    pl.semaphore_wait(barrier, len(NBRS))
 
     def put(buf, r, first, count, y):
         for hf in range(halves):
@@ -122,7 +115,7 @@
                 tile = jnp.concatenate([x_vm[g, hf, :, r, pl.ds(first, imgs)].reshape(block, LANES) for hf in range(halves)], axis=1)
                 y = jnp.dot(perm[...], tile, preferred_element_type=jnp.float32)
                 put(g, r, first, imgs, y.astype(jnp.bfloat16))
-            if i == 2:
+            if i == 1:
                 send(g, ROW_SENDS)
         send(g, COL_SENDS)
     for c in w_copies + [b_copy]:
@@ -142,19 +135,17 @@
             y = conv_row(g, 0, r, 1, cols - 2)
             put(g + GROUPS, r, 1, cols - 2, y.astype(jnp.bfloat16))
         receive(g)
-        for r in (0, rows - 1):
-            y = conv_row(g, 0, r, 0, cols)
-            put(g + GROUPS, r, 0, cols, y.astype(jnp.bfloat16))
-        taps = []
-        for t in range(TAPS):
-            sides = [act[g, pl.ds(1 + t // 3, rows - 2), c + t % 3] for c in (0, cols - 1)]
-            taps.append(jnp.concatenate(sides, axis=0))
-        y = conv(taps, 0).astype(jnp.bfloat16)
-        half = (rows - 2) * imgs
-        for s, c in enumerate((0, cols - 1)):
+        edge = cols * imgs
+        for r, c in ((0, 0), (rows - 1, cols - 1)):
+            taps = []
+            for t in range(TAPS):
+                line = act[g, r + t // 3, pl.ds(t % 3, cols)]
+                side = act[g, pl.ds(1 + t // 3, rows - 2), c + t % 3]
+                taps.append(jnp.concatenate([line, side], axis=0))
+            y = conv(taps, 0).astype(jnp.bfloat16)
+            put(g + GROUPS, r, 0, cols, y[:edge])
             for hf in range(halves):
-                piece = y[s * half:(s + 1) * half, hf * LANES:(hf + 1) * LANES]
-                act[g + GROUPS, pl.ds(2, rows - 2), c + 1, hf] = piece.reshape(rows - 2, imgs, LANES)
+                act[g + GROUPS, pl.ds(2, rows - 2), c + 1, hf] = y[edge:, hf * LANES:(hf + 1) * LANES].reshape(rows - 2, imgs, LANES)
         send(g + GROUPS, ROW_SENDS + COL_SENDS)
         return carry
 
@@ -165,7 +156,7 @@
         for i, r in enumerate(order):
             y = conv_row(p, p // GROUPS, r, 0, cols)
             put(p + GROUPS, r, 0, cols, y.astype(jnp.bfloat16))
-            if i == 2:
+            if i == 1:
                 send(p + GROUPS, ROW_SENDS)
         send(p + GROUPS, COL_SENDS)
         return carry
@@ -190,9 +181,7 @@
 
     def finish(buf, carry):
         for n in range(len(NBRS)):
-            @pl.when(exists(*NBRS[n]))
-            def _(n=n):
-                edge_copy(buf, n).wait_send()
+            edge_copy(buf, n).wait_send()
         return carry
 
     lax.fori_loop(0, layers * GROUPS, finish, 0)
@@ -216,7 +205,7 @@
             in_specs=[hbm, hbm, hbm],
             out_specs=pl.BlockSpec(memory_space=pltpu.VMEM),
             scratch_shapes=[
-                pltpu.VMEM((layers * GROUPS, rows + 2, cols + 2, halves, imgs, LANES), jnp.bfloat16),
+                pltpu.VMEM((layers * GROUPS, rows + 3, cols + 3, halves, imgs, LANES), jnp.bfloat16),
                 pltpu.VMEM((layers, halves, TAPS * ch, LANES), jnp.bfloat16),
                 pltpu.VMEM((layers, ch), jnp.float32),
                 pltpu.VMEM((GROUPS, halves, imgs, rows, cols, LANES), jnp.bfloat16),

time: 60.7 us -> 62.2 us (1.025)
  the two profiles are of different devices: /device:TPU:97 before, /device:TPU:0 now
where the time goes in v3:
time: 62.2 us; the launch traced here: 62.1 us
  Pallas kernels  60.1 us (97%)
  local copies, waits for them, and re-layouts  2.02 us (3%)
    pallas_call x1, Pallas kernels, local_stack(): pl.pallas_call(functools.partial(kernel, dims), out_shape=pltpu.VMEM((bat...  60.1 us
    unnamed x1, local copies, waits for them, and re-layouts  2.02 us

profile of v3, /device:TPU:0, one launch (start us, length us, event | category | flops | bytes accessed | tf_op | source)
XLA Modules:
  0.0 62.1 jit_solution(13586542145059027324)
XLA Ops:
  0.0 60.1 %conv_stack.1 = bf16[32,8,32,256]{3,2,1,0:T(8,128)(2,1)S(1)} custom-call(bf16[32,8,32,256]{3,2,1,0:T(8,128)(2,1)} %x_hbm.1, bf16[4,2304,256]{2,1,0:T(8,128)(2,1)} %bitcast.1, f32[4,256]{1,0:T(4,128)} %b_hbm.1), custom_call_target="tpu_custom_call" | custom-call | tf_op jit(solution)/shard_map/conv_stack/pallas_call | solution.py:202
  60.1 2.0 %copy.5 = bf16[32,8,32,256]{3,2,1,0:T(8,128)(2,1)} copy(bf16[32,8,32,256]{3,2,1,0:T(8,128)(2,1)S(1)} %conv_stack.1) | data formatting | bytes 8388608

commit v4 on v3

--- a/solution.py
+++ b/solution.py
@@ -22,24 +22,26 @@
     pitch = cols + 8
     row, col = lax.axis_index("row"), lax.axis_index("col")
 
-    def span(step, size, at, devs):
+    has = {(-1, 0): row > 0, (1, 0): row < row_devs - 1, (0, -1): col > 0, (0, 1): col < col_devs - 1}
+
+    def exists(dr, dc):
+        if dr and dc:
+            return jnp.logical_and(has[(dr, 0)], has[(0, dc)])
+        return has[(dr, dc)]
+
+    def span(step, size):
         if step < 0:
-            return pl.ds(1, 1), pl.ds(jnp.where(at == 0, size + 2, size + 1), 1), lax.rem(at + devs - 1, devs)
+            return pl.ds(1, 1), pl.ds(size + 1, 1)
         if step > 0:
-            return pl.ds(size, 1), pl.ds(jnp.where(at == devs - 1, size + 2, 0), 1), lax.rem(at + 1, devs)
-        return pl.ds(1, size), pl.ds(1, size), at
-
-    spans = {}
-    for step in (-1, 0, 1):
-        spans["row", step] = span(step, rows, row, row_devs)
-        spans["col", step] = span(step, cols, col, col_devs)
+            return pl.ds(size, 1), pl.ds(0, 1)
+        return pl.ds(1, size), pl.ds(1, size)
 
     def neighbour(n):
-        return {"row": spans["row", NBRS[n][0]][2], "col": spans["col", NBRS[n][1]][2]}
+        return {"row": row + NBRS[n][0], "col": col + NBRS[n][1]}
 
     def edge_copy(buf, n):
-        src_r, dst_r, _ = spans["row", NBRS[n][0]]
-        src_c, dst_c, _ = spans["col", NBRS[n][1]]
+        src_r, dst_r = span(NBRS[n][0], rows)
+        src_c, dst_c = span(NBRS[n][1], cols)
         return pltpu.make_async_remote_copy(
             src_ref=act.at[buf, src_r, src_c],
             dst_ref=act.at[buf, dst_r, dst_c],
@@ -51,11 +53,15 @@
 
     def send(buf, which):
         for n in which:
-            edge_copy(buf, n).start()
+            @pl.when(exists(*NBRS[n]))
+            def _(n=n):
+                edge_copy(buf, n).start()
 
     def receive(buf):
-        for n in range(len(NBRS)):
-            edge_copy(buf, n).wait_recv()
+        for n, (dr, dc) in enumerate(NBRS):
+            @pl.when(exists(-dr, -dc))
+            def _(n=n):
+                edge_copy(buf, n).wait_recv()
 
     x_copies, w_copies = [], []
     for g in range(GROUPS):
@@ -67,12 +73,14 @@
             w_copies.append(pltpu.make_async_copy(
                 w_hbm.at[l, :, pl.ds(hf * LANES, LANES)], w_vm.at[l, hf], in_sem.at[(GROUPS + l) * halves + hf]))
     b_copy = pltpu.make_async_copy(b_hbm, b_ref, in_sem.at[(GROUPS + layers) * halves])
-    for c in x_copies + w_copies + [b_copy]:
+    for c in x_copies[:halves]:
         c.start()
 
     barrier = pltpu.get_barrier_semaphore()
     for n in range(len(NBRS)):
-        pl.semaphore_signal(barrier, inc=1, device_id=neighbour(n), device_id_type=MESH)
+        @pl.when(exists(*NBRS[n]))
+        def _(n=n):
+            pl.semaphore_signal(barrier, inc=1, device_id=neighbour(n), device_id_type=MESH)
 
     def zero_borders(buf, carry):
         @pl.when(row == 0)
@@ -100,7 +108,9 @@
     swapped = (out_row % imgs) * imgs + out_row // imgs
     perm[...] = jnp.where(in_row == swapped, 1.0, 0.0).astype(jnp.bfloat16)
 
-    pl.semaphore_wait(barrier, len(NBRS))
+    n_row = 1 + sum(has[(d, 0)].astype(jnp.int32) for d in (-1, 1))
+    n_col = 1 + sum(has[(0, d)].astype(jnp.int32) for d in (-1, 1))
+    pl.semaphore_wait(barrier, n_row * n_col - 1)
 
     def put(buf, r, first, count, y):
         for hf in range(halves):
@@ -110,6 +120,9 @@
     for g in range(GROUPS):
         for hf in range(halves):
             x_copies[g * halves + hf].wait()
+        if g == 0:
+            for c in x_copies[halves:] + w_copies + [b_copy]:
+                c.start()
         for i, r in enumerate(order):
             for first in range(0, cols, imgs):
                 tile = jnp.concatenate([x_vm[g, hf, :, r, pl.ds(first, imgs)].reshape(block, LANES) for hf in range(halves)], axis=1)
@@ -181,7 +194,9 @@
 
     def finish(buf, carry):
         for n in range(len(NBRS)):
-            edge_copy(buf, n).wait_send()
+            @pl.when(exists(*NBRS[n]))
+            def _(n=n):
+                edge_copy(buf, n).wait_send()
         return carry
 
     lax.fori_loop(0, layers * GROUPS, finish, 0)
@@ -205,7 +220,7 @@
             in_specs=[hbm, hbm, hbm],
             out_specs=pl.BlockSpec(memory_space=pltpu.VMEM),
             scratch_shapes=[
-                pltpu.VMEM((layers * GROUPS, rows + 3, cols + 3, halves, imgs, LANES), jnp.bfloat16),
+                pltpu.VMEM((layers * GROUPS, rows + 2, cols + 2, halves, imgs, LANES), jnp.bfloat16),
                 pltpu.VMEM((layers, halves, TAPS * ch, LANES), jnp.bfloat16),
                 pltpu.VMEM((layers, ch), jnp.float32),
                 pltpu.VMEM((GROUPS, halves, imgs, rows, cols, LANES), jnp.bfloat16),

time: 62.2 us -> 55.5 us (0.89)
  the two profiles are of different devices: /device:TPU:0 before, /device:TPU:97 now
where the time goes in v4:
time: 55.5 us; the launch traced here: 55.4 us
  Pallas kernels  53.4 us (96%)
  local copies, waits for them, and re-layouts  2.02 us (4%)
    pallas_call x1, Pallas kernels, local_stack(): pl.pallas_call(functools.partial(kernel, dims), out_shape=pltpu.VMEM((bat...  53.4 us
    unnamed x1, local copies, waits for them, and re-layouts  2.02 us

profile of v4, /device:TPU:97, one launch (start us, length us, event | category | flops | bytes accessed | tf_op | source)
XLA Modules:
  0.0 55.4 jit_solution(4427515073315486324)
XLA Ops:
  0.0 53.4 %conv_stack.1 = bf16[32,8,32,256]{3,2,1,0:T(8,128)(2,1)S(1)} custom-call(bf16[32,8,32,256]{3,2,1,0:T(8,128)(2,1)} %x_hbm.1, bf16[4,2304,256]{2,1,0:T(8,128)(2,1)} %bitcast.1, f32[4,256]{1,0:T(4,128)} %b_hbm.1), custom_call_target="tpu_custom_call" | custom-call | tf_op jit(solution)/shard_map/conv_stack/pallas_call | solution.py:217
  53.4 2.0 %copy.5 = bf16[32,8,32,256]{3,2,1,0:T(8,128)(2,1)} copy(bf16[32,8,32,256]{3,2,1,0:T(8,128)(2,1)S(1)} %conv_stack.1) | data formatting | bytes 8388608

commit v5 on v4

--- a/solution.py
+++ b/solution.py
@@ -12,8 +12,8 @@
 GROUPS = 2
 TAPS = 9
 NBRS = ((-1, 0), (1, 0), (0, -1), (0, 1), (-1, -1), (-1, 1), (1, -1), (1, 1))
-ROW_SENDS = (0, 1, 4, 5, 6, 7)
-COL_SENDS = (2, 3)
+SEND_ORDER = (4, 5, 6, 7, 2, 3, 0, 1)
+EARLY_ROWS = 2
 
 
 def kernel(dims, x_hbm, w_hbm, b_hbm, o_ref, act, w_vm, b_ref, x_vm, perm, turn, in_sem, send_sem, recv_sem):
@@ -51,8 +51,8 @@
             device_id_type=MESH,
         )
 
-    def send(buf, which):
-        for n in which:
+    def send(buf):
+        for n in SEND_ORDER:
             @pl.when(exists(*NBRS[n]))
             def _(n=n):
                 edge_copy(buf, n).start()
@@ -73,7 +73,7 @@
             w_copies.append(pltpu.make_async_copy(
                 w_hbm.at[l, :, pl.ds(hf * LANES, LANES)], w_vm.at[l, hf], in_sem.at[(GROUPS + l) * halves + hf]))
     b_copy = pltpu.make_async_copy(b_hbm, b_ref, in_sem.at[(GROUPS + layers) * halves])
-    for c in x_copies[:halves]:
+    for c in x_copies[:halves] + w_copies[:halves] + [b_copy]:
         c.start()
 
     barrier = pltpu.get_barrier_semaphore()
@@ -108,31 +108,23 @@
     swapped = (out_row % imgs) * imgs + out_row // imgs
     perm[...] = jnp.where(in_row == swapped, 1.0, 0.0).astype(jnp.bfloat16)
 
-    n_row = 1 + sum(has[(d, 0)].astype(jnp.int32) for d in (-1, 1))
-    n_col = 1 + sum(has[(0, d)].astype(jnp.int32) for d in (-1, 1))
-    pl.semaphore_wait(barrier, n_row * n_col - 1)
+    for c in x_copies[halves:]:
+        c.start()
 
     def put(buf, r, first, count, y):
         for hf in range(halves):
             act[buf, r + 1, pl.ds(first + 1, count), hf] = y[:, hf * LANES:(hf + 1) * LANES].reshape(count, imgs, LANES)
 
     order = (0, rows - 1) + tuple(range(1, rows - 1))
-    for g in range(GROUPS):
+
+    def turn_input(g):
         for hf in range(halves):
             x_copies[g * halves + hf].wait()
-        if g == 0:
-            for c in x_copies[halves:] + w_copies + [b_copy]:
-                c.start()
-        for i, r in enumerate(order):
+        for r in order:
             for first in range(0, cols, imgs):
                 tile = jnp.concatenate([x_vm[g, hf, :, r, pl.ds(first, imgs)].reshape(block, LANES) for hf in range(halves)], axis=1)
                 y = jnp.dot(perm[...], tile, preferred_element_type=jnp.float32)
                 put(g, r, first, imgs, y.astype(jnp.bfloat16))
-            if i == 1:
-                send(g, ROW_SENDS)
-        send(g, COL_SENDS)
-    for c in w_copies + [b_copy]:
-        c.wait()
 
     def conv(taps, layer):
         lhs = jnp.concatenate([tap[..., hf, :, :].reshape(-1, LANES) for tap in taps for hf in range(halves)], axis=1)
@@ -143,54 +135,92 @@
     def conv_row(p, layer, r, first, count):
         return conv([act[p, r + t // 3, pl.ds(first + t % 3, count)] for t in range(TAPS)], layer)
 
-    def first_layer(g, carry):
-        for r in range(1, rows - 1):
-            y = conv_row(g, 0, r, 1, cols - 2)
-            put(g + GROUPS, r, 1, cols - 2, y.astype(jnp.bfloat16))
-        receive(g)
+    def keep(buf, r, first, count, y):
+        put(buf, r, first, count, y.astype(jnp.bfloat16))
+
+    def keep_last(buf, r, first, count, y):
+        for i in range(count):
+            for hf in range(halves):
+                turn[buf - layers * GROUPS, r, hf, pl.ds(first + i, imgs, stride=pitch), :] = y[i * imgs:(i + 1) * imgs, hf * LANES:(hf + 1) * LANES]
+
+    def write_row(g, r):
+        for i in range(imgs):
+            for hf in range(halves):
+                line = turn[g, r, hf, pl.ds(i * pitch, cols), :].astype(jnp.bfloat16)
+                o_ref[g * imgs + i, r, :, pl.ds(hf * LANES, LANES)] = line
+
+    def interior(p, which, store):
+        for r in which:
+            store(p + GROUPS, r, 1, cols - 2, conv_row(p, p // GROUPS, r, 1, cols - 2))
+
+    def side_taps(p, c):
+        return [act[p, pl.ds(1 + t // 3, rows - 2), c + t % 3] for t in range(TAPS)]
+
+    inner = range(1, rows - 1)
+    corners = ((0, 0), (rows - 1, cols - 1))
+
+    def edges(p):
         edge = cols * imgs
-        for r, c in ((0, 0), (rows - 1, cols - 1)):
-            taps = []
-            for t in range(TAPS):
-                line = act[g, r + t // 3, pl.ds(t % 3, cols)]
-                side = act[g, pl.ds(1 + t // 3, rows - 2), c + t % 3]
-                taps.append(jnp.concatenate([line, side], axis=0))
-            y = conv(taps, 0).astype(jnp.bfloat16)
-            put(g + GROUPS, r, 0, cols, y[:edge])
+        for r, c in corners:
+            side = side_taps(p, c)
+            taps = [jnp.concatenate([act[p, r + t // 3, pl.ds(t % 3, cols)], side[t]], axis=0) for t in range(TAPS)]
+            y = conv(taps, p // GROUPS).astype(jnp.bfloat16)
+            put(p + GROUPS, r, 0, cols, y[:edge])
             for hf in range(halves):
-                act[g + GROUPS, pl.ds(2, rows - 2), c + 1, hf] = y[edge:, hf * LANES:(hf + 1) * LANES].reshape(rows - 2, imgs, LANES)
-        send(g + GROUPS, ROW_SENDS + COL_SENDS)
-        return carry
-
-    lax.fori_loop(0, GROUPS, first_layer, 0)
-
-    def middle_layer(p, carry):
+                act[p + GROUPS, pl.ds(2, rows - 2), c + 1, hf] = y[edge:, hf * LANES:(hf + 1) * LANES].reshape(rows - 2, imgs, LANES)
+
+    turn_input(0)
+    turn_input(1)
+    for c in w_copies[:halves] + [b_copy]:
+        c.wait()
+    interior(0, inner[:EARLY_ROWS], keep)
+    n_row = 1 + sum(has[(d, 0)].astype(jnp.int32) for d in (-1, 1))
+    n_col = 1 + sum(has[(0, d)].astype(jnp.int32) for d in (-1, 1))
+    pl.semaphore_wait(barrier, n_row * n_col - 1)
+    for g in range(GROUPS):
+        send(g)
+    for c in w_copies[halves:]:
+        c.start()
+    interior(0, inner[EARLY_ROWS:], keep)
+    interior(1, inner, keep)
+    for c in w_copies[halves:]:
+        c.wait()
+
+    def middle(p, carry):
         receive(p)
-        for i, r in enumerate(order):
-            y = conv_row(p, p // GROUPS, r, 0, cols)
-            put(p + GROUPS, r, 0, cols, y.astype(jnp.bfloat16))
-            if i == 1:
-                send(p + GROUPS, ROW_SENDS)
-        send(p + GROUPS, COL_SENDS)
-        return carry
-
-    lax.fori_loop(GROUPS, (layers - 1) * GROUPS, middle_layer, 0)
-
-    def last_layer(g, carry):
+        edges(p)
+        send(p + GROUPS)
+        interior(p + GROUPS, inner, keep)
+        return carry
+
+    lax.fori_loop(0, (layers - 2) * GROUPS, middle, 0)
+
+    def next_to_last(p, carry):
+        receive(p)
+        edges(p)
+        send(p + GROUPS)
+        interior(p + GROUPS, inner, keep_last)
+        return carry
+
+    lax.fori_loop((layers - 2) * GROUPS, (layers - 1) * GROUPS, next_to_last, 0)
+
+    def last(g, carry):
         p = (layers - 1) * GROUPS + g
         receive(p)
-        for r in range(rows):
-            y = conv_row(p, layers - 1, r, 0, cols)
-            for c in range(cols):
-                for hf in range(halves):
-                    turn[r % 2, hf, pl.ds(c, imgs, stride=pitch), :] = y[c * imgs:(c + 1) * imgs, hf * LANES:(hf + 1) * LANES]
-            for i in range(imgs):
-                for hf in range(halves):
-                    line = turn[r % 2, hf, pl.ds(i * pitch, cols), :].astype(jnp.bfloat16)
-                    o_ref[g * imgs + i, r, :, pl.ds(hf * LANES, LANES)] = line
-        return carry
-
-    lax.fori_loop(0, GROUPS, last_layer, 0)
+        for _, c in corners:
+            y = conv(side_taps(p, c), layers - 1)
+            for i in range(rows - 2):
+                keep_last(p + GROUPS, i + 1, c, 1, y[i * imgs:(i + 1) * imgs])
+        for r, _ in corners:
+            keep_last(p + GROUPS, r, 0, cols, conv_row(p, layers - 1, r, 0, cols))
+            if r == 0:
+                for i in inner:
+                    write_row(g, i)
+        for r, _ in corners:
+            write_row(g, r)
+        return carry
+
+    lax.fori_loop(0, GROUPS, last, 0)
 
     def finish(buf, carry):
         for n in range(len(NBRS)):
@@ -225,7 +255,7 @@
                 pltpu.VMEM((layers, ch), jnp.float32),
                 pltpu.VMEM((GROUPS, halves, imgs, rows, cols, LANES), jnp.bfloat16),
                 pltpu.VMEM((imgs * imgs, imgs * imgs), jnp.bfloat16),
-                pltpu.VMEM((2, halves, imgs * (cols + 8), LANES), jnp.float32),
+                pltpu.VMEM((GROUPS, rows, halves, imgs * (cols + 8), LANES), jnp.float32),
                 pltpu.SemaphoreType.DMA(((GROUPS + layers) * halves + 1,)),
                 pltpu.SemaphoreType.DMA((layers * GROUPS, len(NBRS))),
                 pltpu.SemaphoreType.DMA((layers * GROUPS, len(NBRS))),

time: 55.5 us -> 51.5 us (0.928)
  Pallas kernels: 53.4 us -> 48.9 us
    pallas_call x1, Pallas kernels: 53.4 us -> 48.9 us  [local_stack(): pl.pallas_call(functools.partial(kernel, dims), out_shape=pltpu.VMEM((bat...]
where the time goes in v5:
time: 51.5 us; the launch traced here: 50.9 us
  Pallas kernels  48.9 us (95%)
  local copies, waits for them, and re-layouts  2.02 us (4%)
    pallas_call x1, Pallas kernels, local_stack(): pl.pallas_call(functools.partial(kernel, dims), out_shape=pltpu.VMEM((bat...  48.9 us
    unnamed x1, local copies, waits for them, and re-layouts  2.02 us

profile of v5, /device:TPU:97, one launch (start us, length us, event | category | flops | bytes accessed | tf_op | source)
XLA Modules:
  0.0 50.9 jit_solution(16917624063642467788)
XLA Ops:
  0.0 48.9 %conv_stack.1 = bf16[32,8,32,256]{3,2,1,0:T(8,128)(2,1)S(1)} custom-call(bf16[32,8,32,256]{3,2,1,0:T(8,128)(2,1)} %x_hbm.1, bf16[4,2304,256]{2,1,0:T(8,128)(2,1)} %bitcast.1, f32[4,256]{1,0:T(4,128)} %b_hbm.1), custom_call_target="tpu_custom_call" | custom-call | tf_op jit(solution)/shard_map/conv_stack/pallas_call | solution.py:247
  48.9 2.0 %copy.5 = bf16[32,8,32,256]{3,2,1,0:T(8,128)(2,1)} copy(bf16[32,8,32,256]{3,2,1,0:T(8,128)(2,1)S(1)} %conv_stack.1) | data formatting | bytes 8388608

commit v6 on v5

--- a/solution.py
+++ b/solution.py
@@ -19,7 +19,7 @@
 def kernel(dims, x_hbm, w_hbm, b_hbm, o_ref, act, w_vm, b_ref, x_vm, perm, turn, in_sem, send_sem, recv_sem):
     layers, imgs, rows, cols, ch, row_devs, col_devs = dims
     halves = ch // LANES
-    pitch = cols + 8
+    pitch = cols + 1
     row, col = lax.axis_index("row"), lax.axis_index("col")
 
     has = {(-1, 0): row > 0, (1, 0): row < row_devs - 1, (0, -1): col > 0, (0, 1): col < col_devs - 1}
@@ -255,7 +255,7 @@
                 pltpu.VMEM((layers, ch), jnp.float32),
                 pltpu.VMEM((GROUPS, halves, imgs, rows, cols, LANES), jnp.bfloat16),
                 pltpu.VMEM((imgs * imgs, imgs * imgs), jnp.bfloat16),
-                pltpu.VMEM((GROUPS, rows, halves, imgs * (cols + 8), LANES), jnp.float32),
+                pltpu.VMEM((GROUPS, rows, halves, imgs * (cols + 1), LANES), jnp.float32),
                 pltpu.SemaphoreType.DMA(((GROUPS + layers) * halves + 1,)),
                 pltpu.SemaphoreType.DMA((layers * GROUPS, len(NBRS))),
                 pltpu.SemaphoreType.DMA((layers * GROUPS, len(NBRS))),

time: 51.5 us -> 50.7 us (0.984)
  Pallas kernels: 48.9 us -> 48 us
    pallas_call x1, Pallas kernels: 48.9 us -> 48 us  [local_stack(): pl.pallas_call(functools.partial(kernel, dims), out_shape=pltpu.VMEM((bat...]
where the time goes in v6:
time: 50.7 us; the launch traced here: 50 us
  Pallas kernels  48 us (95%)
  local copies, waits for them, and re-layouts  2.02 us (4%)
    pallas_call x1, Pallas kernels, local_stack(): pl.pallas_call(functools.partial(kernel, dims), out_shape=pltpu.VMEM((bat...  48 us
    unnamed x1, local copies, waits for them, and re-layouts  2.02 us

profile of v6, /device:TPU:97, one launch (start us, length us, event | category | flops | bytes accessed | tf_op | source)
XLA Modules:
  0.0 50.0 jit_solution(15537127073369776641)
XLA Ops:
  0.0 48.0 %conv_stack.1 = bf16[32,8,32,256]{3,2,1,0:T(8,128)(2,1)S(1)} custom-call(bf16[32,8,32,256]{3,2,1,0:T(8,128)(2,1)} %x_hbm.1, bf16[4,2304,256]{2,1,0:T(8,128)(2,1)} %bitcast.1, f32[4,256]{1,0:T(4,128)} %b_hbm.1), custom_call_target="tpu_custom_call" | custom-call | tf_op jit(solution)/shard_map/conv_stack/pallas_call | solution.py:247
  48.0 2.0 %copy.5 = bf16[32,8,32,256]{3,2,1,0:T(8,128)(2,1)} copy(bf16[32,8,32,256]{3,2,1,0:T(8,128)(2,1)S(1)} %conv_stack.1) | data formatting | bytes 8388608

commit v7 on v6

--- a/solution.py
+++ b/solution.py
@@ -16,10 +16,59 @@
 EARLY_ROWS = 2
 
 
-def kernel(dims, x_hbm, w_hbm, b_hbm, o_ref, act, w_vm, b_ref, x_vm, perm, turn, in_sem, send_sem, recv_sem):
+def row_taps(act, p, r, first, count):
+    return [act[p, r + t // 3, pl.ds(first + t % 3, count)] for t in range(TAPS)]
+
+
+def conv_dot(taps, w_vm, b_ref, layer, b_layer):
+    halves = w_vm.shape[1]
+    lhs = jnp.concatenate([tap[..., hf, :, :].reshape(-1, LANES) for tap in taps for hf in range(halves)], axis=1)
+    wt = jnp.concatenate([w_vm[layer, hf] for hf in range(halves)], axis=1)
+    y = jnp.dot(lhs, wt, preferred_element_type=jnp.float32)
+    return jnp.maximum(y + b_ref[pl.ds(b_layer, 1), :], 0.0)
+
+
+def keep_lines(lines, imgs, first, count, y):
+    halves, length = lines.shape[:2]
+    pitch = length // imgs
+    for i in range(count):
+        for hf in range(halves):
+            lines[hf, pl.ds(first + i, imgs, stride=pitch), :] = y[i * imgs:(i + 1) * imgs, hf * LANES:(hf + 1) * LANES]
+
+
+def write_lines(o_ref, lines, first_img, imgs, r):
+    halves, length = lines.shape[:2]
+    pitch, cols = length // imgs, o_ref.shape[2]
+    for i in range(imgs):
+        for hf in range(halves):
+            line = lines[hf, pl.ds(i * pitch, cols), :].astype(jnp.bfloat16)
+            o_ref[first_img + i, r, :, pl.ds(hf * LANES, LANES)] = line
+
+
+def last_row(dims, done, act, w_vm, b_ref, o_hbm, lines, stage, sem):
+    layers, imgs, rows, cols, ch = dims[:5]
+    first_img = (GROUPS - 1) * imgs
+    copies = []
+    for g in range(GROUPS):
+        count = rows if g < GROUPS - 1 else rows - 1
+        where = (pl.ds(g * imgs, imgs), pl.ds(0, count))
+        copies.append(pltpu.make_async_copy(done.at[where], o_hbm.at[where], sem.at[g]))
+    for c in copies:
+        c.start()
+    half = cols // 2
+    for first in (0, half):
+        y = conv_dot(row_taps(act, 0, 0, first, half), w_vm, b_ref, 0, layers - 1)
+        keep_lines(lines, imgs, first, half, y)
+    write_lines(stage, lines, 0, imgs, 0)
+    tail = pltpu.make_async_copy(stage, o_hbm.at[pl.ds(first_img, imgs), pl.ds(rows - 1, 1)], sem.at[GROUPS])
+    tail.start()
+    for c in copies + [tail]:
+        c.wait()
+
+
+def kernel(dims, x_hbm, w_hbm, b_hbm, o_ref, act_end, w_end, b_ref, act, w_vm, x_vm, perm, turn, in_sem, send_sem, recv_sem):
     layers, imgs, rows, cols, ch, row_devs, col_devs = dims
     halves = ch // LANES
-    pitch = cols + 1
     row, col = lax.axis_index("row"), lax.axis_index("col")
 
     has = {(-1, 0): row > 0, (1, 0): row < row_devs - 1, (0, -1): col > 0, (0, 1): col < col_devs - 1}
@@ -72,7 +121,10 @@
         for hf in range(halves):
             w_copies.append(pltpu.make_async_copy(
                 w_hbm.at[l, :, pl.ds(hf * LANES, LANES)], w_vm.at[l, hf], in_sem.at[(GROUPS + l) * halves + hf]))
-    b_copy = pltpu.make_async_copy(b_hbm, b_ref, in_sem.at[(GROUPS + layers) * halves])
+    for hf in range(halves):
+        w_copies.append(pltpu.make_async_copy(
+            w_hbm.at[layers - 1, :, pl.ds(hf * LANES, LANES)], w_end.at[0, hf], in_sem.at[(GROUPS + layers) * halves + hf]))
+    b_copy = pltpu.make_async_copy(b_hbm, b_ref, in_sem.at[(GROUPS + layers + 1) * halves])
     for c in x_copies[:halves] + w_copies[:halves] + [b_copy]:
         c.start()
 
@@ -127,27 +179,19 @@
                 put(g, r, first, imgs, y.astype(jnp.bfloat16))
 
     def conv(taps, layer):
-        lhs = jnp.concatenate([tap[..., hf, :, :].reshape(-1, LANES) for tap in taps for hf in range(halves)], axis=1)
-        wt = jnp.concatenate([w_vm[layer, hf] for hf in range(halves)], axis=1)
-        y = jnp.dot(lhs, wt, preferred_element_type=jnp.float32)
-        return jnp.maximum(y + b_ref[pl.ds(layer, 1), :], 0.0)
+        return conv_dot(taps, w_vm, b_ref, layer, layer)
 
     def conv_row(p, layer, r, first, count):
-        return conv([act[p, r + t // 3, pl.ds(first + t % 3, count)] for t in range(TAPS)], layer)
+        return conv(row_taps(act, p, r, first, count), layer)
 
     def keep(buf, r, first, count, y):
         put(buf, r, first, count, y.astype(jnp.bfloat16))
 
     def keep_last(buf, r, first, count, y):
-        for i in range(count):
-            for hf in range(halves):
-                turn[buf - layers * GROUPS, r, hf, pl.ds(first + i, imgs, stride=pitch), :] = y[i * imgs:(i + 1) * imgs, hf * LANES:(hf + 1) * LANES]
+        keep_lines(turn.at[buf - layers * GROUPS, r], imgs, first, count, y)
 
     def write_row(g, r):
-        for i in range(imgs):
-            for hf in range(halves):
-                line = turn[g, r, hf, pl.ds(i * pitch, cols), :].astype(jnp.bfloat16)
-                o_ref[g * imgs + i, r, :, pl.ds(hf * LANES, LANES)] = line
+        write_lines(o_ref, turn.at[g, r], g * imgs, imgs, r)
 
     def interior(p, which, store):
         for r in which:
@@ -170,9 +214,9 @@
                 act[p + GROUPS, pl.ds(2, rows - 2), c + 1, hf] = y[edge:, hf * LANES:(hf + 1) * LANES].reshape(rows - 2, imgs, LANES)
 
     turn_input(0)
-    turn_input(1)
     for c in w_copies[:halves] + [b_copy]:
         c.wait()
+    turn_input(1)
     interior(0, inner[:EARLY_ROWS], keep)
     n_row = 1 + sum(has[(d, 0)].astype(jnp.int32) for d in (-1, 1))
     n_col = 1 + sum(has[(0, d)].astype(jnp.int32) for d in (-1, 1))
@@ -204,23 +248,32 @@
 
     lax.fori_loop((layers - 2) * GROUPS, (layers - 1) * GROUPS, next_to_last, 0)
 
-    def last(g, carry):
-        p = (layers - 1) * GROUPS + g
+    def sides(p):
         receive(p)
         for _, c in corners:
             y = conv(side_taps(p, c), layers - 1)
             for i in range(rows - 2):
                 keep_last(p + GROUPS, i + 1, c, 1, y[i * imgs:(i + 1) * imgs])
+
+    end = layers * GROUPS
+    for p in range(end - GROUPS, end - 1):
+        g = p - (end - GROUPS)
+        sides(p)
         for r, _ in corners:
             keep_last(p + GROUPS, r, 0, cols, conv_row(p, layers - 1, r, 0, cols))
             if r == 0:
                 for i in inner:
                     write_row(g, i)
-        for r, _ in corners:
-            write_row(g, r)
-        return carry
-
-    lax.fori_loop(0, GROUPS, last, 0)
+    sides(end - 1)
+    for r, _ in corners:
+        write_row(0, r)
+    act_end[0] = act[end - 1, pl.ds(rows - 1, 3)]
+    half = cols // 2
+    for first in (0, half):
+        keep_last(end - 1 + GROUPS, 0, first, half, conv_row(end - 1, layers - 1, 0, first, half))
+    for i in inner:
+        write_row(GROUPS - 1, i)
+    write_row(GROUPS - 1, 0)
 
     def finish(buf, carry):
         for n in range(len(NBRS)):
@@ -244,24 +297,43 @@
         halves = ch // LANES
         dims = (layers, imgs, rows, cols, ch, row_devs, col_devs)
         hbm = pl.BlockSpec(memory_space=pltpu.HBM)
-        return pl.pallas_call(
+        vmem = pl.BlockSpec(memory_space=pltpu.VMEM)
+        pitch = cols + 1
+        done, act_end, w_end, b_vm = pl.pallas_call(
             functools.partial(kernel, dims),
-            out_shape=pltpu.VMEM((batch, rows, cols, ch), jnp.bfloat16),
+            out_shape=[
+                pltpu.VMEM((batch, rows, cols, ch), jnp.bfloat16),
+                pltpu.VMEM((1, 3, cols + 2, halves, imgs, LANES), jnp.bfloat16),
+                pltpu.VMEM((1, halves, TAPS * ch, LANES), jnp.bfloat16),
+                pltpu.VMEM((layers, ch), jnp.float32),
+            ],
             in_specs=[hbm, hbm, hbm],
-            out_specs=pl.BlockSpec(memory_space=pltpu.VMEM),
+            out_specs=[vmem] * 4,
             scratch_shapes=[
                 pltpu.VMEM((layers * GROUPS, rows + 2, cols + 2, halves, imgs, LANES), jnp.bfloat16),
                 pltpu.VMEM((layers, halves, TAPS * ch, LANES), jnp.bfloat16),
-                pltpu.VMEM((layers, ch), jnp.float32),
                 pltpu.VMEM((GROUPS, halves, imgs, rows, cols, LANES), jnp.bfloat16),
                 pltpu.VMEM((imgs * imgs, imgs * imgs), jnp.bfloat16),
-                pltpu.VMEM((GROUPS, rows, halves, imgs * (cols + 1), LANES), jnp.float32),
-                pltpu.SemaphoreType.DMA(((GROUPS + layers) * halves + 1,)),
+                pltpu.VMEM((GROUPS, rows, halves, imgs * pitch, LANES), jnp.float32),
+                pltpu.SemaphoreType.DMA(((GROUPS + layers + 1) * halves + 1,)),
                 pltpu.SemaphoreType.DMA((layers * GROUPS, len(NBRS))),
                 pltpu.SemaphoreType.DMA((layers * GROUPS, len(NBRS))),
             ],
-            compiler_params=pltpu.CompilerParams(collective_id=0, has_side_effects=True, vmem_limit_bytes=56 * 1024 * 1024),
+            compiler_params=pltpu.CompilerParams(collective_id=0, has_side_effects=True, vmem_limit_bytes=55 * 1024 * 1024),
             name="conv_stack",
         )(x_tile, weights.reshape(layers, TAPS * ch, ch), biases)
+        return pl.pallas_call(
+            functools.partial(last_row, dims),
+            out_shape=jax.ShapeDtypeStruct((batch, rows, cols, ch), jnp.bfloat16),
+            in_specs=[vmem] * 4,
+            out_specs=hbm,
+            scratch_shapes=[
+                pltpu.VMEM((halves, imgs * pitch, LANES), jnp.float32),
+                pltpu.VMEM((imgs, 1, cols, ch), jnp.bfloat16),
+                pltpu.SemaphoreType.DMA((GROUPS + 1,)),
+            ],
+            compiler_params=pltpu.CompilerParams(vmem_limit_bytes=16 * 1024 * 1024),
+            name="last_row",
+        )(done, act_end, w_end, b_vm)
 
     return jax.shard_map(local_stack, mesh=mesh, in_specs=(act_spec, P(), P()), out_specs=act_spec, check_vma=False)

time: 50.7 us -> 50.2 us (level)
  local copies, waits for them, and re-layouts: 2.02 us -> 0 us
  Pallas kernels: 48 us -> 49.4 us
    unnamed x1 -> x0, local copies, waits for them, and re-layouts: 2.02 us -> none
    pallas_call x1 -> x2, Pallas kernels: 48 us -> 49.4 us  [the longest x1 47.3 us: local_stack(): pl.pallas_call(functools.partial(kernel, dims), out_shape=[pltpu.VMEM((ba...]
where the time goes in v7:
time: 50.2 us; the launch traced here: 49.5 us
  Pallas kernels  49.4 us (98%)
    pallas_call x1, Pallas kernels, local_stack(): pl.pallas_call(functools.partial(kernel, dims), out_shape=[pltpu.VMEM((ba...  47.3 us
    pallas_call x1, Pallas kernels, local_stack(): pl.pallas_call(functools.partial(last_row, dims), out_shape=jax.ShapeDtyp...  2.03 us

profile of v7, /device:TPU:97, one launch (start us, length us, event | category | flops | bytes accessed | tf_op | source)
XLA Modules:
  0.0 49.5 jit_solution(16542843971804259517)
XLA Ops:
  0.0 47.3 %conv_stack.1 = (bf16[32,8,32,256]{3,2,1,0:T(8,128)(2,1)S(1)}, bf16[1,3,34,2,16,128]{5,4,3,2,1,0:T(8,128)(2,1)S(1)}, bf16[1,2,2304,128]{3,2,1,0:T(8,128)(2,1)S(1)}, f32[4,256]{1,0:T(4,128)S(1)}) custom-call(bf16[32,8,32,256]{3,2,1,0:T(8,128)(2,1)} %x_hbm.1, bf16[4,2304,256]{2,1,0:T(8,128)(2,1)} %bitcast.1, f32[4,256]{1,0:T(4,128)} %b_hbm.1), custom_call_target="tpu_custom_call" | custom-call | tf_op jit(solution)/shard_map/conv_stack/pallas_call | solution.py:302
  47.3 2.0 %last_row.1 = bf16[32,8,32,256]{3,2,1,0:T(8,128)(2,1)} custom-call(bf16[32,8,32,256]{3,2,1,0:T(8,128)(2,1)S(1)} %get-tuple-element.9.done, bf16[1,3,34,2,16,128]{5,4,3,2,1,0:T(8,128)(2,1)S(1)} %get-tuple-element.10.act, bf16[1,2,2304,128]{3,2,1,0:T(8,128)(2,1)S(1)} %get-tuple-element.11.w_vm, f32[4,256]{1,0:T(4,128)S(1)} %get-tuple-element.12.b_ref), custom_call_target="tpu_custom_call" | custom-call | tf_op jit(solution)/shard_map/last_row/pallas_call | solution.py:325

commit v8 on v7

--- a/solution.py
+++ b/solution.py
@@ -13,7 +13,6 @@
 TAPS = 9
 NBRS = ((-1, 0), (1, 0), (0, -1), (0, 1), (-1, -1), (-1, 1), (1, -1), (1, 1))
 SEND_ORDER = (4, 5, 6, 7, 2, 3, 0, 1)
-EARLY_ROWS = 2
 
 
 def row_taps(act, p, r, first, count):
@@ -125,7 +124,7 @@
         w_copies.append(pltpu.make_async_copy(
             w_hbm.at[layers - 1, :, pl.ds(hf * LANES, LANES)], w_end.at[0, hf], in_sem.at[(GROUPS + layers) * halves + hf]))
     b_copy = pltpu.make_async_copy(b_hbm, b_ref, in_sem.at[(GROUPS + layers + 1) * halves])
-    for c in x_copies[:halves] + w_copies[:halves] + [b_copy]:
+    for c in x_copies:
         c.start()
 
     barrier = pltpu.get_barrier_semaphore()
@@ -160,7 +159,7 @@
     swapped = (out_row % imgs) * imgs + out_row // imgs
     perm[...] = jnp.where(in_row == swapped, 1.0, 0.0).astype(jnp.bfloat16)
 
-    for c in x_copies[halves:]:
+    for c in w_copies[:halves] + [b_copy]:
         c.start()
 
     def put(buf, r, first, count, y):
@@ -214,10 +213,9 @@
                 act[p + GROUPS, pl.ds(2, rows - 2), c + 1, hf] = y[edge:, hf * LANES:(hf + 1) * LANES].reshape(rows - 2, imgs, LANES)
 
     turn_input(0)
+    turn_input(1)
     for c in w_copies[:halves] + [b_copy]:
         c.wait()
-    turn_input(1)
-    interior(0, inner[:EARLY_ROWS], keep)
     n_row = 1 + sum(has[(d, 0)].astype(jnp.int32) for d in (-1, 1))
     n_col = 1 + sum(has[(0, d)].astype(jnp.int32) for d in (-1, 1))
     pl.semaphore_wait(barrier, n_row * n_col - 1)
@@ -225,7 +223,7 @@
         send(g)
     for c in w_copies[halves:]:
         c.start()
-    interior(0, inner[EARLY_ROWS:], keep)
+    interior(0, inner, keep)
     interior(1, inner, keep)
     for c in w_copies[halves:]:
         c.wait()

time: 50.2 us -> 49.9 us (level); the launches traced: 49.5 us -> 49.8 us
  no operation moved by 1% of the time
where the time goes in v8:
time: 49.9 us; the launch traced here: 49.8 us
  Pallas kernels  49.6 us (99%)
    pallas_call x1, Pallas kernels, local_stack(): pl.pallas_call(functools.partial(kernel, dims), out_shape=[pltpu.VMEM((ba...  47.6 us
    pallas_call x1, Pallas kernels, local_stack(): pl.pallas_call(functools.partial(last_row, dims), out_shape=jax.ShapeDtyp...  2.03 us

profile of v8, /device:TPU:97, one launch (start us, length us, event | category | flops | bytes accessed | tf_op | source)
XLA Modules:
  0.0 49.8 jit_solution(5598106872270584385)
XLA Ops:
  0.0 47.6 %conv_stack.1 = (bf16[32,8,32,256]{3,2,1,0:T(8,128)(2,1)S(1)}, bf16[1,3,34,2,16,128]{5,4,3,2,1,0:T(8,128)(2,1)S(1)}, bf16[1,2,2304,128]{3,2,1,0:T(8,128)(2,1)S(1)}, f32[4,256]{1,0:T(4,128)S(1)}) custom-call(bf16[32,8,32,256]{3,2,1,0:T(8,128)(2,1)} %x_hbm.1, bf16[4,2304,256]{2,1,0:T(8,128)(2,1)} %bitcast.1, f32[4,256]{1,0:T(4,128)} %b_hbm.1), custom_call_target="tpu_custom_call" | custom-call | tf_op jit(solution)/shard_map/conv_stack/pallas_call | solution.py:300
  47.6 2.0 %last_row.1 = bf16[32,8,32,256]{3,2,1,0:T(8,128)(2,1)} custom-call(bf16[32,8,32,256]{3,2,1,0:T(8,128)(2,1)S(1)} %get-tuple-element.9.done, bf16[1,3,34,2,16,128]{5,4,3,2,1,0:T(8,128)(2,1)S(1)} %get-tuple-element.10.act, bf16[1,2,2304,128]{3,2,1,0:T(8,128)(2,1)S(1)} %get-tuple-element.11.w_vm, f32[4,256]{1,0:T(4,128)S(1)} %get-tuple-element.12.b_ref), custom_call_target="tpu_custom_call" | custom-call | tf_op jit(solution)/shard_map/last_row/pallas_call | solution.py:323
